TPU v7x, 32 devices: a whole 2x2x4 slice. The times are simulated.
32 devices in a mesh: items: 2 (over x), rows: 16 (over z, y, core).
Axes of the slice: x: 2, y: 2, z: 4, core: 2. Of those that a mesh axis runs over, the one named last changes fastest.
Arguments:
- patches: bfloat16 [128, 32, 1152], P(('items', 'rows')), may hold values from -6 to 6
- condition: bfloat16 [4, 1152], P('items'), may hold values from -6 to 6
- lengths: int32 [4], P('items'), may hold values from 256 to 1024, as said below
- modulator: bfloat16 [1152, 6912], P(None, 'rows'), may hold values from -0.1875 to 0.1875
- baseline: float32 [6912], P('rows'), may hold values from -4 to 4
- projector: bfloat16 [1152, 3456], P('rows'), may hold values from -0.1875 to 0.1875
- forgetter: bfloat16 [1152, 16], P('rows'), may hold values from -0.1875 to 0.1875
- retention: float32 [16], replicated, may hold values from 0.5 to 5
- smoother: float32 [9, 1152], replicated, may hold values from -6 to 6
- pedestal: float32 [1152], replicated, may hold values from -16 to 16
- combiner: bfloat16 [1152, 1152], P('rows'), may hold values from -0.005859375 to 0.005859375
- displacement: float32 [1152], replicated, may hold values from -4 to 4
- expander: bfloat16 [1152, 4608], P('rows'), may hold values from -0.1875 to 0.1875
- thresholds: float32 [4608], replicated, may hold values from -4 to 4
- reducer: bfloat16 [4608, 1152], P('rows'), may hold values from -0.09375 to 0.09375
- leveling: float32 [1152], replicated, may hold values from -4 to 4
- cotangent: bfloat16 [128, 32, 1152], P(('items', 'rows')), may hold values from -6 to 6
Outputs:
- block_output: bfloat16 [128, 32, 1152], P(('items', 'rows'))
- patches_grad: bfloat16 [128, 32, 1152], P(('items', 'rows'))
- condition_grad: float32 [4, 1152], P('items')
- modulator_grad: float32 [1152, 6912], P(None, 'rows')
- baseline_grad: float32 [6912], P('rows')
- projector_grad: float32 [1152, 3456], P('rows')
- forgetter_grad: float32 [1152, 16], P('rows')
- retention_grad: float32 [16], replicated
- smoother_grad: float32 [9, 1152], replicated
- pedestal_grad: float32 [1152], replicated
- combiner_grad: float32 [1152, 1152], P('rows')
- displacement_grad: float32 [1152], replicated
- expander_grad: float32 [1152, 4608], P('rows')
- thresholds_grad: float32 [4608], replicated
- reducer_grad: float32 [4608, 1152], P('rows')
- leveling_grad: float32 [1152], replicated
Inputs may be any that keep to these rules, and one draw needn't show every extreme that they name: lengths[b] counts the valid patches of item b, the first ones in row-major place; in every draw some item has all 1024 valid.
All inputs are finite; a program needn't handle non-finite values.
Results may differ from a plain program's by a relative error of at most 0.018.
Values may be sent and summed in bfloat16 or wider, within the bound.
A program may use at most 256 MiB of HBM per device.

v0:
```python
import jax
import jax.numpy as jnp
from jax import lax
from jax.sharding import PartitionSpec as P

H = 16
HD = 72
D = 1152
GRID = 32
PATCHES = 1024
TRACT = 64
ROWS_DEV = 4
TOK_DEV = 128


EPS = 1e-06
HIGH = lax.Precision.HIGHEST


def modulate(values, offset, stretch):
    centred = values - jnp.mean(values, axis=-1, keepdims=True)
    spread = jnp.mean(centred * centred, axis=-1, keepdims=True)
    return centred * lax.rsqrt(spread + EPS) * (1.0 + stretch) + offset


def tract_step(carried, pieces):
    queries, key_rows, values, decays = pieces
    length = queries.shape[1]
    summed = jnp.cumsum(decays, axis=1)
    totals = summed[:, -1]
    factor = queries.shape[-1] ** (-0.5)
    scores = jnp.einsum("bik,bjk->bij", queries, key_rows, precision=HIGH)
    causal = jnp.arange(length)[:, None] >= jnp.arange(length)[None, :]
    offsets = jnp.where(causal, summed[:, :, None] - summed[:, None, :], 0.0)
    weights = jnp.where(causal, jnp.exp(offsets), 0.0)
    inside = jnp.einsum("bij,bjv->biv", scores * weights, values, precision=HIGH)
    carried_in = (
        jnp.einsum("bik,bkv->biv", queries, carried, precision=HIGH) * jnp.exp(summed)[:, :, None]
    )
    outputs = (inside + carried_in) * factor
    fading = jnp.exp(totals[:, None] - summed)[:, :, None]
    carried_next = jnp.exp(totals)[:, None, None] * carried + jnp.einsum(
        "bjk,bjv->bkv", key_rows * fading, values, precision=HIGH
    )
    return (carried_next, outputs)


def outer_sum(left, right):
    return lax.dot_general(
        left, right, (((0,), (0,)), ((), ())), preferred_element_type=jnp.float32
    )


def back_dot(gradient, matrix):
    return lax.dot_general(
        gradient, matrix, (((1,), (1,)), ((), ())), preferred_element_type=jnp.float32
    )


def to_tracts(source):
    leading = source.shape[0]
    turned = jnp.swapaxes(source, 1, 2)
    shaped = turned.reshape((leading, PATCHES // TRACT, TRACT) + source.shape[3:])
    return jnp.moveaxis(shaped, 1, 0)


def from_tracts(source):
    leading = source.shape[1]
    shaped = jnp.moveaxis(source, 0, 1).reshape((leading, GRID, GRID) + source.shape[3:])
    return jnp.swapaxes(shaped, 1, 2)


def pad_cells(grid):
    return jnp.pad(grid, ((0, 0), (1, 1), (1, 1), (0, 0)))


def smooth_cells(grid, kernel, offset):
    padded = pad_cells(grid)
    result = jnp.zeros_like(grid) + offset[:, None, None, :]
    for tap_index in range(9):
        down_by = tap_index // 3
        right_by = tap_index % 3
        result = (
            result
            + kernel[tap_index][:, None, None, :]
            * padded[:, down_by : down_by + GRID, right_by : right_by + GRID]
        )
    return result


def on_device(
    patches,
    condition,
    lengths,
    modulator,
    baseline,
    projector,
    forgetter,
    retention,
    smoother,
    pedestal,
    combiner,
    displacement,
    expander,
    thresholds,
    reducer,
    leveling,
    cotangent,
):
    devices = lax.axis_size("rows")
    device_index = lax.axis_index("rows")
    items_here = condition.shape[0]
    blocks_per = GRID // ROWS_DEV
    item_local = device_index // blocks_per
    position = device_index % blocks_per
    heads_split = devices // H
    width_split = D // devices
    squashed = jax.nn.silu(condition.astype(jnp.float32)).astype(jnp.bfloat16)
    modulation_piece = (
        (jnp.dot(squashed, modulator, preferred_element_type=jnp.float32) + baseline)
        .astype(jnp.bfloat16)
        .T
    )
    modulation_all, combiner_all, expander_all, reducer_all = (
        lax.all_gather(modulation_piece, "rows", axis=0, tiled=True),
        lax.all_gather(combiner, "rows", axis=0, tiled=True),
        lax.all_gather(expander, "rows", axis=0, tiled=True),
        lax.all_gather(reducer, "rows", axis=0, tiled=True),
    )
    modulation = lax.dynamic_index_in_dim(modulation_all, item_local, 1, keepdims=False).astype(
        jnp.float32
    )
    shift_one = modulation[0:D]
    scale_one = modulation[D : 2 * D]
    gate_one = modulation[2 * D : 3 * D]
    shift_two = modulation[3 * D : 4 * D]
    scale_two = modulation[4 * D : 5 * D]
    gate_two = modulation[5 * D : 6 * D]
    inputs = patches.astype(jnp.float32).reshape(TOK_DEV, D)
    hidden = modulate(inputs, shift_one, scale_one).astype(jnp.bfloat16)
    pieces = (
        lax.all_gather(projector, "rows", axis=0, tiled=True),
        lax.all_gather(forgetter, "rows", axis=0, tiled=True),
    )
    projected = jnp.dot(hidden, pieces[0], preferred_element_type=jnp.float32)
    forget_logit = jnp.dot(hidden, pieces[1], preferred_element_type=jnp.float32)
    forget_logit = forget_logit + retention
    decays = (jax.nn.log_sigmoid(forget_logit) / 16.0).astype(jnp.bfloat16)
    row_start = position * ROWS_DEV
    places = (row_start + jnp.arange(ROWS_DEV, dtype=jnp.int32)[:, None]) * GRID + jnp.arange(
        GRID, dtype=jnp.int32
    )[None, :]
    validity = (places < lengths[item_local]).reshape(TOK_DEV, 1)
    projected_low = projected.astype(jnp.bfloat16)
    queries = projected_low[:, :D]
    key_rows = jnp.where(validity, projected_low[:, D : 2 * D], jnp.zeros_like(queries))
    values = jnp.where(validity, projected_low[:, 2 * D :], jnp.zeros_like(queries))

    def spread(source):
        grouped = source.reshape(TOK_DEV, H, 1, HD)
        return jnp.broadcast_to(grouped, (TOK_DEV, H, heads_split, HD)).reshape(
            TOK_DEV, devices, HD
        )

    outgoing = jnp.concatenate(
        [spread(queries), spread(key_rows), values.reshape(TOK_DEV, devices, width_split)], axis=2
    )
    outgoing = jnp.swapaxes(outgoing, 0, 1)
    decay_parts = (
        jnp.broadcast_to(decays.reshape(TOK_DEV, H, 1), (TOK_DEV, H, heads_split))
        .reshape(TOK_DEV, devices)
        .T
    )
    incoming, decays_in = (
        lax.all_to_all(outgoing, "rows", split_axis=0, concat_axis=0, tiled=True),
        lax.all_to_all(decay_parts, "rows", split_axis=0, concat_axis=0, tiled=True),
    )
    column_data = to_tracts(incoming.reshape(items_here, GRID, GRID, incoming.shape[-1]))
    column_decay = to_tracts(decays_in.reshape(items_here, GRID, GRID))
    initial = jnp.zeros((items_here, HD, width_split), jnp.float32)
    channel_start = device_index * width_split
    kernel = lax.dynamic_slice_in_dim(smoother, channel_start, width_split, 1)[:, None, :]
    offset = lax.dynamic_slice_in_dim(pedestal, channel_start, width_split, 0)[None, :]

    def forward_block(carried, pieces):
        block_data, block_decay = pieces
        as_float = block_data.astype(jnp.float32)
        carried_next, outputs = tract_step(
            carried,
            (
                as_float[..., :HD],
                as_float[..., HD : 2 * HD],
                as_float[..., 2 * HD :],
                block_decay.astype(jnp.float32),
            ),
        )
        return (carried_next, (outputs.astype(jnp.bfloat16), carried))

    last_state, (attended_tracts, states_in) = lax.scan(
        forward_block, initial, (column_data, column_decay)
    )
    attended_grid = from_tracts(attended_tracts).astype(jnp.float32)
    smoothed_cols = smooth_cells(attended_grid, kernel, offset).astype(jnp.bfloat16)
    returned = lax.all_to_all(
        smoothed_cols.reshape(devices, TOK_DEV, width_split),
        "rows",
        split_axis=0,
        concat_axis=0,
        tiled=True,
    )
    smoothed = jnp.swapaxes(returned, 0, 1).reshape(TOK_DEV, D)
    branch = jnp.dot(smoothed, combiner_all, preferred_element_type=jnp.float32) + displacement
    middle = inputs + gate_one * branch
    hidden_two = modulate(middle, shift_two, scale_two).astype(jnp.bfloat16)
    expanded = jnp.dot(hidden_two, expander_all, preferred_element_type=jnp.float32) + thresholds
    activated = jax.nn.gelu(expanded, approximate=True).astype(jnp.bfloat16)
    reduced = jnp.dot(activated, reducer_all, preferred_element_type=jnp.float32) + leveling
    block_output = (middle + gate_two * reduced).astype(jnp.bfloat16).reshape(ROWS_DEV, GRID, D)
    combiner_all, expander_all, reducer_all, projector_all, forgetter_all = (
        lax.all_gather(combiner, "rows", axis=0, tiled=True),
        lax.all_gather(expander, "rows", axis=0, tiled=True),
        lax.all_gather(reducer, "rows", axis=0, tiled=True),
        lax.all_gather(projector, "rows", axis=0, tiled=True),
        lax.all_gather(forgetter, "rows", axis=0, tiled=True),
    )
    upstream = cotangent.astype(jnp.float32).reshape(TOK_DEV, D)
    gate_two_grad = jnp.sum(upstream * reduced, axis=0)
    reduced_grad = (gate_two * upstream).astype(jnp.bfloat16)
    reducer_grad = outer_sum(activated, reduced_grad)
    leveling_grad = jnp.sum(reduced_grad.astype(jnp.float32), axis=0)
    activated_grad = back_dot(reduced_grad, reducer_all)
    activation_pull = jax.vjp(lambda values_in: jax.nn.gelu(values_in, approximate=True), expanded)[
        1
    ]
    expanded_grad = activation_pull(activated_grad)[0].astype(jnp.bfloat16)
    expander_grad = outer_sum(hidden_two, expanded_grad)
    thresholds_grad = jnp.sum(expanded_grad.astype(jnp.float32), axis=0)
    hidden_two_grad = back_dot(expanded_grad, expander_all)
    second_pull = jax.vjp(modulate, middle, shift_two, scale_two)[1]
    middle_part, shift_two_grad, scale_two_grad = second_pull(hidden_two_grad)
    middle_grad = upstream + middle_part
    gate_one_grad = jnp.sum(middle_grad * branch, axis=0)
    branch_grad = (gate_one * middle_grad).astype(jnp.bfloat16)
    combiner_grad = outer_sum(smoothed, branch_grad)
    displacement_grad = jnp.sum(branch_grad.astype(jnp.float32), axis=0)
    smoothed_grad = back_dot(branch_grad, combiner_all).astype(jnp.bfloat16)
    combiner_share, expander_share, reducer_share = (
        lax.psum_scatter(combiner_grad, "rows", scatter_dimension=0, tiled=True),
        lax.psum_scatter(expander_grad, "rows", scatter_dimension=0, tiled=True),
        lax.psum_scatter(reducer_grad, "rows", scatter_dimension=0, tiled=True),
    )
    pedestal_grad = jnp.sum(smoothed_grad.astype(jnp.float32), axis=0)
    smoothed_low = smoothed_grad.reshape(TOK_DEV, devices, width_split)
    returned_grad = lax.all_to_all(
        jnp.swapaxes(smoothed_low, 0, 1), "rows", split_axis=0, concat_axis=0, tiled=True
    )
    grad_grid = returned_grad.reshape(items_here, GRID, GRID, width_split)
    grad_float = grad_grid.astype(jnp.float32)
    grad_padded = pad_cells(grad_float)
    attended_padded = pad_cells(attended_grid)
    tap_grads = []
    attended_grad = jnp.zeros_like(grad_float)
    for tap_index in range(9):
        down_by = tap_index // 3
        right_by = tap_index % 3
        tap_grads.append(
            jnp.sum(
                grad_float
                * attended_padded[:, down_by : down_by + GRID, right_by : right_by + GRID],
                axis=(1, 2),
            )
        )
        attended_grad = (
            attended_grad
            + kernel[tap_index][:, None, None, :]
            * grad_padded[:, 2 - down_by : 2 - down_by + GRID, 2 - right_by : 2 - right_by + GRID]
        )
    tap_stack = jnp.stack(tap_grads)
    tap_stack = jnp.sum(tap_stack, axis=1)
    smoother_grad = lax.dynamic_update_slice(
        jnp.zeros((9, D), jnp.float32), tap_stack, (jnp.int32(0), channel_start)
    )
    grad_tracts = to_tracts(attended_grad.astype(jnp.bfloat16))

    def backward_block(carried_grad, pieces):
        block_data, block_decay, block_grad, carried = pieces
        as_float = block_data.astype(jnp.float32)
        inputs_tuple = (
            as_float[..., :HD],
            as_float[..., HD : 2 * HD],
            as_float[..., 2 * HD :],
            block_decay.astype(jnp.float32),
        )
        step_pull = jax.vjp(tract_step, carried, inputs_tuple)[1]
        carried_back, pieces_back = step_pull((carried_grad, block_grad.astype(jnp.float32)))
        query_grad, key_grad, value_grad, decay_grad = pieces_back
        return (
            carried_back,
            (jnp.concatenate([query_grad, key_grad, value_grad], axis=-1), decay_grad),
        )

    final_grad, (data_grad, decay_grads) = lax.scan(
        backward_block,
        jnp.zeros_like(initial),
        (column_data, column_decay, grad_tracts, states_in),
        reverse=True,
    )
    sending = from_tracts(data_grad).reshape(devices, TOK_DEV, data_grad.shape[-1])
    sending_decay = from_tracts(decay_grads).reshape(devices, TOK_DEV)
    arrived, arrived_decay = (
        lax.all_to_all(
            sending.astype(jnp.bfloat16), "rows", split_axis=0, concat_axis=0, tiled=True
        ).astype(sending.dtype),
        lax.all_to_all(
            sending_decay.astype(jnp.bfloat16), "rows", split_axis=0, concat_axis=0, tiled=True
        ).astype(sending_decay.dtype),
    )
    query_back = jnp.swapaxes(
        jnp.sum(arrived[..., :HD].reshape(H, heads_split, TOK_DEV, HD), axis=1), 0, 1
    ).reshape(TOK_DEV, D)
    key_back = jnp.swapaxes(
        jnp.sum(arrived[..., HD : 2 * HD].reshape(H, heads_split, TOK_DEV, HD), axis=1), 0, 1
    ).reshape(TOK_DEV, D)
    value_back = jnp.swapaxes(arrived[..., 2 * HD :], 0, 1).reshape(TOK_DEV, D)
    decay_back = jnp.sum(arrived_decay.reshape(H, heads_split, TOK_DEV), axis=1).T
    key_back = jnp.where(validity, key_back, 0.0)
    value_back = jnp.where(validity, value_back, 0.0)
    projected_grad = jnp.concatenate([query_back, key_back, value_back], axis=1).astype(
        jnp.bfloat16
    )
    forget_grad = (decay_back * jax.nn.sigmoid(-forget_logit) / 16.0).astype(jnp.bfloat16)
    retention_grad = jnp.sum(forget_grad.astype(jnp.float32), axis=0)
    projector_grad = outer_sum(hidden, projected_grad)
    forgetter_grad = outer_sum(hidden, forget_grad)
    hidden_grad = back_dot(projected_grad, projector_all) + back_dot(forget_grad, forgetter_all)
    first_pull = jax.vjp(modulate, inputs, shift_one, scale_one)[1]
    inputs_part, shift_one_grad, scale_one_grad = first_pull(hidden_grad)
    patches_grad = (middle_grad + inputs_part).astype(jnp.bfloat16).reshape(ROWS_DEV, GRID, D)
    modulation_grad = jnp.concatenate(
        [
            shift_one_grad,
            scale_one_grad,
            gate_one_grad,
            shift_two_grad,
            scale_two_grad,
            gate_two_grad,
        ]
    )
    selector = (jnp.arange(items_here) == item_local).astype(jnp.float32)
    modulation_grid = modulation_grad[:, None] * selector[None, :]
    projector_share, forgetter_share, modulation_share = (
        lax.psum_scatter(projector_grad, "rows", scatter_dimension=0, tiled=True),
        lax.psum_scatter(forgetter_grad, "rows", scatter_dimension=0, tiled=True),
        lax.psum_scatter(modulation_grid, "rows", scatter_dimension=0, tiled=True),
    )
    modulation_rows = modulation_share.T
    modulator_grad = jnp.dot(squashed.astype(jnp.float32).T, modulation_rows, precision=HIGH)
    baseline_grad = jnp.sum(modulation_rows, axis=0)
    squashed_grad = jnp.dot(modulation_rows, modulator.astype(jnp.float32).T, precision=HIGH)
    (
        squashed_sum,
        retention_sum,
        smoother_sum,
        pedestal_sum,
        displacement_sum,
        thresholds_sum,
        leveling_sum,
    ) = lax.psum(
        (
            squashed_grad,
            retention_grad,
            smoother_grad,
            pedestal_grad,
            displacement_grad,
            thresholds_grad,
            leveling_grad,
        ),
        "rows",
    )
    silu_pull = jax.vjp(jax.nn.silu, condition.astype(jnp.float32))[1]
    condition_grad = silu_pull(squashed_sum)[0]
    results = (
        lax.psum(modulator_grad.astype(jnp.bfloat16), "items").astype(jnp.float32),
        lax.psum(baseline_grad.astype(jnp.bfloat16), "items").astype(jnp.float32),
        lax.psum(projector_share.astype(jnp.bfloat16), "items").astype(jnp.float32),
        lax.psum(forgetter_share.astype(jnp.bfloat16), "items").astype(jnp.float32),
        lax.psum(retention_sum.astype(jnp.bfloat16), "items").astype(jnp.float32),
        lax.psum(smoother_sum.astype(jnp.bfloat16), "items").astype(jnp.float32),
        lax.psum(pedestal_sum.astype(jnp.bfloat16), "items").astype(jnp.float32),
        lax.psum(combiner_share.astype(jnp.bfloat16), "items").astype(jnp.float32),
        lax.psum(displacement_sum.astype(jnp.bfloat16), "items").astype(jnp.float32),
        lax.psum(expander_share.astype(jnp.bfloat16), "items").astype(jnp.float32),
        lax.psum(thresholds_sum.astype(jnp.bfloat16), "items").astype(jnp.float32),
        lax.psum(reducer_share.astype(jnp.bfloat16), "items").astype(jnp.float32),
        lax.psum(leveling_sum.astype(jnp.bfloat16), "items").astype(jnp.float32),
    )
    return (
        block_output,
        patches_grad,
        condition_grad,
        results[0],
        results[1],
        results[2],
        results[3],
        results[4],
        results[5],
        results[6],
        results[7],
        results[8],
        results[9],
        results[10],
        results[11],
        results[12],
    )


def solution(mesh):
    in_specs = (
        P(("items", "rows"), None, None),
        P("items", None),
        P("items"),
        P(None, "rows"),
        P("rows"),
        P("rows", None),
        P("rows", None),
        P(),
        P(),
        P(),
        P("rows", None),
        P(),
        P("rows", None),
        P(),
        P("rows", None),
        P(),
        P(("items", "rows"), None, None),
    )
    out_specs = (
        P(("items", "rows"), None, None),
        P(("items", "rows"), None, None),
        P("items", None),
        P(None, "rows"),
        P("rows"),
        P("rows", None),
        P("rows", None),
        P(),
        P(),
        P(),
        P("rows", None),
        P(),
        P("rows", None),
        P(),
        P("rows", None),
        P(),
    )
    return jax.shard_map(
        on_device, mesh=mesh, in_specs=in_specs, out_specs=out_specs, check_vma=False
    )
```

profile of v0, /device:TPU:0, one launch (start us, length us, event | category | flops | bytes accessed | tf_op | source)
XLA Modules:
  0.0 1415.4 jit_solution(18202919970072790144)
XLA Ops:
  10.6 23.7 %all-gather = bf16[16,432,2]{1,2,0:T(2,128)(2,1)S(1)} all-gather(bf16[1,432,2]{1,2,0:T(2,128)(2,1)S(1)} %fusion.104), channel_id=1, replica_groups=mesh['items'=2,'rows'=16] {'rows'}, dimensions={0}, use_global_device_ids=true | all-gather | bytes 29376 | tf_op jit(solution)/shard_map/all_gather | solution.py:125
  35.0 18.0 %all-gather.1 = bf16[16,72,16]{1,2,0:T(8,128)(2,1)S(1)} all-gather(bf16[1,72,16]{1,2,0:T(8,128)(2,1)S(1)} %bitcast.330), channel_id=1, replica_groups=mesh['items'=2,'rows'=16] {'rows'}, dimensions={0}, use_global_device_ids=true | all-gather | bytes 39168 | tf_op jit(solution)/shard_map/all_gather | solution.py:143
  54.4 3.5 all-to-all-start
  59.3 25.6 %all-gather.7.cloned.1.call-done = bf16[1152,3456]{1,0:T(8,128)(2,1)} async-done(((bf16[72,3456]{1,0:T(8,128)(2,1)}), bf16[1152,3456]{1,0:T(8,128)(2,1)}) %all-gather.7.cloned.1.call-update) | async-done | bytes 7962640 | tf_op jit(solution)/shard_map/all_gather | solution.py:142
  84.9 4.7 convolution_convert_fusion
  93.0 3.6 all-to-all-start.1
  99.4 20.6 %all-to-all-done.1 = bf16[16,128,216]{1,2,0:T(8,128)(2,1)S(1)} async-done(((bf16[16,128,216]{1,2,0:T(8,128)(2,1)}), bf16[16,128,216]{1,2,0:T(8,128)(2,1)S(1)}, u32[]{:S(2)}, u32[]{:S(2)}) %all-to-all-start.1) | async-done | bytes 884768 | tf_op jit(solution)/shard_map/all_to_all | solution.py:175
  120.0 1.3 copy.262
  121.3 1.8 copy.263
  124.2 58.6 %while.34 = (s32[]{:T(128)}, f32[2,72,72]{2,1,0:T(8,128)S(1)}, bf16[16,2,64,72]{3,2,0,1:T(8,128)(2,1)}, f32[16,2,72,72]{3,2,1,0:T(8,128)}, bf16[16,2,64]{2,1,0:T...) while((s32[]{:T(128)}, f32[2,72,72]{2,1,0:T(8,128)S(1)}, ...), condition=%wide.region_4.5_spmd.clone, body=%wide.region_2.4_spmd.clone.sunk | while | flops 24335108 | bytes 821685 | solution.py:199
  185.9 2.0 copy.268
  187.8 12.6 all-to-all-start.2
  201.3 14.3 %all-to-all-done.2 = bf16[16,128,72]{1,2,0:T(8,128)(2,1)S(1)} async-done(((bf16[16,128,72]{1,2,0:T(8,128)(2,1)}), bf16[16,128,72]{1,2,0:T(8,128)(2,1)S(1)}, u32[]{:S(2)}, u32[]{:S(2)}) %all-to-all-start.2) | async-done | bytes 294944 | tf_op jit(solution)/shard_map/all_to_all | solution.py:204
  216.3 3.3 fusion.170
  219.9 9.9 all-gather.13.cloned.1.call-done
  229.8 9.0 fusion.173
  238.8 80.4 %all-gather.11.cloned.1.call-done = bf16[1152,4608]{1,0:T(8,128)(2,1)} async-done(((bf16[72,4608]{1,0:T(8,128)(2,1)}), bf16[1152,4608]{1,0:T(8,128)(2,1)}) %all-gather.11.cloned.1.call-update) | async-done | bytes 10616848 | tf_op jit(solution)/shard_map/all_gather | solution.py:127
  319.2 9.3 convert_reduce_fusion
  328.5 3.5 multiply_reduce_fusion.10
  334.0 1.6 convert_reduce_fusion.4
  335.6 1.8 copy.269
  337.5 4.4 all-to-all-start.3
  341.9 10.5 all-to-all-done.3
  352.4 2.2 copy.270
  354.6 3.2 multiply_reduce_fusion.1
  359.9 141.3 %while.35 = (s32[]{:T(128)}, f32[2,72,72]{2,1,0:T(8,128)S(1)}, bf16[16,2,64,216]{3,2,0,1:T(8,128)(2,1)}, bf16[16,2,64]{2,1,0:T(2,128)(2,1)S(1)}, bf16[16,2,64]{2...) while((s32[]{:T(128)}, f32[2,72,72]{2,1,0:T(8,128)S(1)}, ...), condition=%wide.region_18.19_spmd.clone, body=%wide.region_9.18_spmd.clone.sunk | while | flops 69959680 | bytes 1926470 | solution.py:302
  366.1 1.2 fusion.268
  383.7 1.2 fusion.268
  392.6 1.2 fusion.268
  401.4 1.2 fusion.268
  410.2 1.2 fusion.268
  419.0 1.2 fusion.268
  436.7 1.2 fusion.268
  445.5 1.2 fusion.268
  454.4 1.2 fusion.268
  489.7 1.2 fusion.268
  498.5 1.2 fusion.268
  502.0 3.5 all-to-all-start.5
  505.5 1.8 copy.277
  507.3 1.3 copy.278
  508.6 3.2 all-to-all-done.5
  511.8 3.6 all-to-all-start.4
  515.6 20.0 %all-to-all-done.4 = bf16[16,128,216]{1,2,0:T(8,128)(2,1)S(1)} async-done(((bf16[16,128,216]{1,2,0:T(8,128)(2,1)}), bf16[16,128,216]{1,2,0:T(8,128)(2,1)S(1)}, u32[]{:S(2)}, u32[]{:S(2)}) %all-to-all-start.4) | async-done | bytes 884768 | tf_op jit(solution)/shard_map/all_to_all | solution.py:311
  540.3 6.0 fusion.137
  547.7 7.1 fusion.124
  554.9 2.4 copy.297
  558.3 3.2 fusion.175
  562.6 8.4 fusion.136
  571.0 11.7 fusion.165
  583.6 11.8 fusion.166
  597.3 29.3 %reduce-scatter.17.cloned.1.call-done = f32[432,2]{1,0:T(8,128)} async-done(((f32[6912,2]{1,0:T(8,128)}), f32[432,2]{1,0:T(8,128)}) %reduce-scatter.17.cloned.1.call-update) | async-done | bytes 3472
  626.7 2.8 convolution_convert_fusion.1
  629.5 78.1 %reduce-scatter.21.cloned.1.call-done = f32[72,1152]{1,0:T(8,128)} async-done(((f32[1152,1152]{1,0:T(8,128)}), f32[72,1152]{1,0:T(8,128)}) %reduce-scatter.21.cloned.1.call-update) | async-done | bytes 331792
  707.6 1.7 convert_element_type.334
  709.3 171.9 %reduce-scatter.19.cloned.1.call-done = f32[72,3456]{1,0:T(8,128)} async-done(((f32[1152,3456]{1,0:T(8,128)}), f32[72,3456]{1,0:T(8,128)}) %reduce-scatter.19.cloned.1.call-update) | async-done | bytes 995344
  881.2 2.0 convert_element_type.322
  883.3 214.7 %reduce-scatter.13.cloned.1.call-done = f32[72,4608]{1,0:T(8,128)} async-done(((f32[1152,4608]{1,0:T(8,128)}), f32[72,4608]{1,0:T(8,128)}) %reduce-scatter.13.cloned.1.call-update) | async-done | bytes 1327120 | tf_op jit(solution)/shard_map/reduce_scatter | solution.py:249
  1098.0 2.2 convert_element_type.339
  1100.2 214.5 %reduce-scatter.15.cloned.1.call-done = f32[288,1152]{1,0:T(8,128)} async-done(((f32[4608,1152]{1,0:T(8,128)}), f32[288,1152]{1,0:T(8,128)}) %reduce-scatter.15.cloned.1.call-update) | async-done | bytes 1327120 | tf_op jit(solution)/shard_map/reduce_scatter | solution.py:250
  1314.8 2.2 convert_element_type.344
  1318.3 62.0 %all-reduce.13 = (f32[2,1152]{1,0:T(2,128)S(1)}, bf16[1152,16]{0,1:T(8,128)(2,1)S(1)}, bf16[16]{0:T(256)(128)(2,1)S(1)}, bf16[9,1152]{1,0:T(8,128)(2,1)S(1)}, bf...) all-reduce(f32[2,1152]{1,0:T(2,128)S(1)} %fusion.174, ...), channel_id=1, replica_groups=mesh['items'=2,'rows'=16] {'rows'}, use_global_device_ids=true, to_apply=%region_28.29 | all-reduce | flops 39184 | bytes 239712 | tf_op jit(solution)/shard_map/psum | solution.py:368
  1380.5 10.5 all-reduce.7
  1396.3 5.0 all-reduce.12.cloned.1.call-done
  1401.3 2.7 convert_element_type.319
  (778 shorter events, 229.5 us)
Async XLA Ops:
  7.2 2.3 copy-start
  7.2 27.2 %copy-start.1 = (bf16[4,32,1152]{2,1,0:T(8,128)(2,1)S(1)}, bf16[4,32,1152]{2,1,0:T(8,128)(2,1)}, u32[]{:S(2)}) copy-start(bf16[4,32,1152]{2,1,0:T(8,128)(2,1)} %param.21) | copy-start | bytes 884740
  7.2 27.7 %copy-start.28 = (bf16[72,16]{0,1:T(8,128)(2,1)S(1)}, bf16[72,16]{0,1:T(8,128)(2,1)}, u32[]{:S(2)}) copy-start(bf16[72,16]{0,1:T(8,128)(2,1)} %param.27) | copy-start | bytes 6916
  7.2 46.3 %copy-start.31 = (f32[16]{0:T(128)S(1)}, f32[16]{0:T(128)}, u32[]{:S(2)}) copy-start(f32[16]{0:T(128)} %param.28) | copy-start | bytes 196
  7.2 50.6 %copy-start.32 = (s32[2]{0:T(128)S(1)}, s32[2]{0:T(128)}, u32[]{:S(2)}) copy-start(s32[2]{0:T(128)} %param.23) | copy-start | bytes 28
  7.2 77.6 %all-gather.7.cloned.1.call-start = ((), (), s32[]{:S(2)}) async-start(), calls=%async_computation.11 | async-start | bytes 8460288 | tf_op jit(solution)/shard_map/all_gather | solution.py:142
  8.0 193.3 %all-gather.9.cloned.1.call-start = ((), (), s32[]{:S(2)}) async-start(), calls=%async_computation.12 | async-start | bytes 2820096 | tf_op jit(solution)/shard_map/all_gather | solution.py:126
  8.7 221.1 %all-gather.13.cloned.1.call-start = ((), (), s32[]{:S(2)}) async-start(), calls=%async_computation.14 | async-start | bytes 11280384 | tf_op jit(solution)/shard_map/all_gather | solution.py:128
  54.4 38.6 %all-to-all-start = ((bf16[16,1,128]{2,1,0:T(2,128)(2,1)}), bf16[16,1,128]{2,1,0:T(2,128)(2,1)S(1)}, u32[]{:S(2)}, u32[]{:S(2)}) async-start(bf16[16,1,128]{2,1,0:T(2,128)(2,1)} %copy.257), calls=%async_computation | async-start | bytes 16384 | tf_op jit(solution)/shard_map/all_to_all | solution.py:176
  93.0 27.0 %all-to-all-start.1 = ((bf16[16,128,216]{1,2,0:T(8,128)(2,1)}), bf16[16,128,216]{1,2,0:T(8,128)(2,1)S(1)}, u32[]{:S(2)}, u32[]{:S(2)}) async-start(bf16[16,128,216]{1,2,0:T(8,128)(2,1)} %maximum_bitcast_fusion.1), calls=%async_computation.1 | async-start | bytes 1769472 | tf_op jit(solution)/shard_map/all_to_all | solution.py:175
  96.6 222.6 %all-gather.11.cloned.1.call-start = ((), (), s32[]{:S(2)}) async-start(), calls=%async_computation.13 | async-start | bytes 11280384 | tf_op jit(solution)/shard_map/all_gather | solution.py:127
  184.0 16.5 %copy-start.9 = (bf16[4,32,1152]{2,1,0:T(8,128)(2,1)S(1)}, bf16[4,32,1152]{2,1,0:T(8,128)(2,1)}, u32[]{:S(2)}) copy-start(bf16[4,32,1152]{2,1,0:T(8,128)(2,1)} %param.37) | copy-start | bytes 884740
  184.0 32.3 %copy-start.27 = (f32[1152]{0:T(1024)S(1)}, f32[1152]{0:T(1024)}, u32[]{:S(2)}) copy-start(f32[1152]{0:T(1024)} %param.32) | copy-start | bytes 13828
  187.8 27.8 %all-to-all-start.2 = ((bf16[16,128,72]{1,2,0:T(8,128)(2,1)}), bf16[16,128,72]{1,2,0:T(8,128)(2,1)S(1)}, u32[]{:S(2)}, u32[]{:S(2)}) async-start(bf16[16,128,72]{1,2,0:T(8,128)(2,1)} %copy.268), calls=%async_computation.2 | async-start | bytes 589824 | tf_op jit(solution)/shard_map/all_to_all | solution.py:204
  215.6 0.7 copy-start.5
  219.9 99.4 %copy-start.29 = (f32[4608]{0:T(1024)S(1)}, f32[4608]{0:T(1024)}, u32[]{:S(2)}) copy-start(f32[4608]{0:T(1024)} %param.34) | copy-start | bytes 55300
  319.2 9.3 copy-start.3
  328.5 3.5 copy-start.4
  328.5 3.8 copy-start.10
  332.0 2.0 copy-start.2
  332.4 0.8 copy-start.14
  333.2 2.5 copy-start.7
  337.5 15.0 %all-to-all-start.3 = ((bf16[16,128,72]{1,2,0:T(8,128)(2,1)}), bf16[16,128,72]{1,2,0:T(8,128)(2,1)}, u32[]{:S(2)}, u32[]{:S(2)}) async-start(bf16[16,128,72]{1,2,0:T(8,128)(2,1)} %bitcast.323), calls=%async_computation.3 | async-start | bytes 589824 | tf_op jit(solution)/shard_map/all_to_all | solution.py:254
  502.0 9.8 all-to-all-start.5
  511.8 23.9 %all-to-all-start.4 = ((bf16[16,128,216]{1,2,0:T(8,128)(2,1)}), bf16[16,128,216]{1,2,0:T(8,128)(2,1)S(1)}, u32[]{:S(2)}, u32[]{:S(2)}) async-start(bf16[16,128,216]{1,2,0:T(8,128)(2,1)} %copy.278), calls=%async_computation.4 | async-start | bytes 1769472 | tf_op jit(solution)/shard_map/all_to_all | solution.py:311
  515.4 111.2 %reduce-scatter.17.cloned.1.call-start = ((), (), s32[]{:S(2)}) async-start(), calls=%async_computation.17 | async-start | bytes 3760128
  540.3 6.0 copy-start.17
  540.3 6.0 copy-start.19
  540.3 6.9 copy-start.13
  546.3 1.0 copy-start.11
  546.3 1.1 copy-start.15
  546.3 1.3 copy-start.23
  546.3 1.3 copy-start.30
  557.3 1.0 copy-start.6
  557.3 1.0 copy-start.8
  557.3 150.3 %reduce-scatter.21.cloned.1.call-start = ((), (), s32[]{:S(2)}) async-start(), calls=%async_computation.19 | async-start | bytes 5640192
  561.5 1.0 copy-start.18
  561.5 1.0 copy-start.20
  561.5 319.7 %reduce-scatter.19.cloned.1.call-start = ((), (), s32[]{:S(2)}) async-start(), calls=%async_computation.18 | async-start | bytes 16920576
  570.9 527.0 %reduce-scatter.13.cloned.1.call-start = ((), (), s32[]{:S(2)}) async-start(), calls=%async_computation.15 | async-start | bytes 22560768 | tf_op jit(solution)/shard_map/reduce_scatter | solution.py:249
  582.7 1.0 copy-start.12
  582.7 732.0 %reduce-scatter.15.cloned.1.call-start = ((), (), s32[]{:S(2)}) async-start(), calls=%async_computation.16 | async-start | bytes 22560768 | tf_op jit(solution)/shard_map/reduce_scatter | solution.py:250
  595.5 0.7 copy-start.33
  595.5 31.2 %copy-start.26 = (bf16[2,1152]{1,0:T(2,128)(2,1)S(1)}, bf16[2,1152]{1,0:T(2,128)(2,1)}, u32[]{:S(2)}) copy-start(bf16[2,1152]{1,0:T(2,128)(2,1)} %param.22) | copy-start | bytes 13828
  595.5 805.8 %all-reduce.12.cloned.1.call-start = ((), (), s32[]{:S(2)}) async-start(), calls=%async_computation.20 | async-start | bytes 5971968 | tf_op jit(solution)/shard_map/psum | solution.py:383
  1100.2 217.4 %copy-start.16 = (f32[432,2]{1,0:T(8,128)S(1)}, f32[432,2]{1,0:T(8,128)}, u32[]{:S(2)}) copy-start(f32[432,2]{1,0:T(8,128)} %reduce-scatter.17.cloned.1.call-done) | copy-start | bytes 10372
  1401.3 2.7 copy-start.24
  1401.3 3.7 copy-start.25
  1401.3 4.5 copy-start.22
  1404.0 2.9 copy-start.21
Sparse Core Ops, SparseCore 0:
  10.2 74.6 all-gather.6
  87.0 48.3 all-gather.8
  137.7 92.0 all-gather.12
  231.9 87.2 all-gather.10
  557.4 69.2 reduce-scatter.16
  630.6 76.9 reduce-scatter.20
  711.7 169.4 reduce-scatter.18
  885.3 212.6 reduce-scatter.12
  1102.1 212.6 reduce-scatter.14
  1318.4 82.9 all-reduce.11
where the time goes:
time: 1430 us; the launch traced here: 1420 us
  waiting for transfers between devices  901 us (63%)
  matrix products  186 us (13%)
  blocking collectives  114 us (8%)
  other arithmetic  92.5 us (6%)
  local copies, waits for them, and re-layouts  71.8 us (5%)
  starting transfers between devices  31.9 us (2%)
  between operations  16 us (1%)
    unnamed x13, waiting for transfers between devices  282 us
    reduce_scatter x1, waiting for transfers between devices, on_device(): lax.psum_scatter(expander_grad, 'rows', scatter_dimension=0, tiled=True)  215 us
    reduce_scatter x1, waiting for transfers between devices, on_device(): lax.psum_scatter(reducer_grad, 'rows', scatter_dimension=0, tiled=True)  215 us
    all_gather x1, waiting for transfers between devices, on_device(): lax.all_gather(expander, 'rows', axis=0, tiled=True)  80.4 us
    psum x1, blocking collectives, on_device(): lax.psum((squashed_grad, retention_grad, smoother_grad, pedestal_grad, di...  62 us
    dot_general x64, matrix products, tract_step(): jnp.einsum('bik,bkv->biv', queries, carried, precision=HIGH)  54.7 us
    dot_general x5, matrix products, outer_sum(): lax.dot_general(left, right, (((0,), (0,)), ((), ())), preferred_element_...  35.2 us
  transfers between devices with their start and end apart: 16, of which 14 were waited for; matrix products, arithmetic and copies ran while one was open for 11% of the time, Pallas kernels for 0%

commit v1 on v0

v1 whole, which is shorter than its diff:
```python
import functools

import jax
import jax.numpy as jnp
from jax import lax
from jax.experimental import pallas as pl
from jax.experimental.pallas import tpu as pltpu
from jax.sharding import Mesh, PartitionSpec as P

H = 16
HD = 72
D = 1152
FF = 4608
GRID = 32
PATCHES = 1024
ROWS_DEV = 4
TOK_DEV = 128
TEAM = GRID // ROWS_DEV
HEADS = H // TEAM
LANES = 128
WIDE = HEADS * LANES
STRIP = 256

EPS = 1e-06
HIGH = lax.Precision.HIGHEST
F32 = jnp.float32
BF16 = jnp.bfloat16
FACTOR = HD ** (-0.5)


def modulate(values, offset, stretch):
    centred = values - jnp.mean(values, axis=-1, keepdims=True)
    spread = jnp.mean(centred * centred, axis=-1, keepdims=True)
    return centred * lax.rsqrt(spread + EPS) * (1.0 + stretch) + offset


def dot(left, right):
    return jnp.dot(left, right, preferred_element_type=F32)


def outer_sum(left, right):
    return lax.dot_general(left, right, (((0,), (0,)), ((), ())), preferred_element_type=F32)


def back_dot(gradient, matrix):
    return lax.dot_general(gradient, matrix, (((1,), (1,)), ((), ())), preferred_element_type=F32)


def column_place(index):
    return (index & (GRID - 1)) * GRID + (index >> 5)


def strip_weights(start, gcol, grow):
    rows = lax.broadcasted_iota(jnp.int32, (STRIP, PATCHES), 0) + start
    cols = lax.broadcasted_iota(jnp.int32, (STRIP, PATCHES), 1)
    causal = column_place(cols) <= column_place(rows)
    return jnp.exp(jnp.where(causal, gcol - grow, -1e30))


def attend_kernel(q_ref, k_ref, v_ref, gcol_ref, grow_ref, out_ref):
    keys = k_ref[...]
    values = v_ref[...]
    grow = grow_ref[0]

    def strip(number, carry):
        start = pl.multiple_of(number * STRIP, STRIP)
        here = pl.ds(start, STRIP)
        weights = strip_weights(start, gcol_ref[0, here, :], grow)
        scores = back_dot(q_ref[here, :], keys) * weights
        out_ref[here, :] = (dot(scores.astype(BF16), values) * FACTOR).astype(BF16)
        return carry

    lax.fori_loop(0, PATCHES // STRIP, strip, 0)


def attend_back_kernel(
    q_ref, k_ref, v_ref, gcol_ref, grow_ref, do_ref, dq_ref, dk_ref, dv_ref, row_ref, col_ref
):
    keys = k_ref[...]
    values = v_ref[...]
    grow = grow_ref[0]
    dk_ref[...] = jnp.zeros_like(dk_ref)
    dv_ref[...] = jnp.zeros_like(dv_ref)
    col_ref[...] = jnp.zeros_like(col_ref)

    def strip(number, carry):
        start = pl.multiple_of(number * STRIP, STRIP)
        here = pl.ds(start, STRIP)
        queries = q_ref[here, :]
        grads = do_ref[here, :]
        weights = strip_weights(start, gcol_ref[0, here, :], grow)
        scores = back_dot(queries, keys) * weights
        back = back_dot(grads, values)
        pulled = (back * weights).astype(BF16)
        moment = back * scores
        dv_ref[...] += outer_sum(scores.astype(BF16), grads)
        dk_ref[...] += outer_sum(pulled, queries)
        dq_ref[here, :] = dot(pulled, keys) * FACTOR
        row_ref[0, here, :] = jnp.sum(moment, axis=1, keepdims=True) * FACTOR
        col_ref[0] += jnp.sum(moment, axis=0, keepdims=True) * FACTOR
        return carry

    lax.fori_loop(0, PATCHES // STRIP, strip, 0)
    dk_ref[...] *= FACTOR
    dv_ref[...] *= FACTOR


def head_specs():
    return [
        pl.BlockSpec((PATCHES, LANES), lambda h: (0, h)),
        pl.BlockSpec((PATCHES, LANES), lambda h: (0, HEADS + h)),
        pl.BlockSpec((PATCHES, LANES), lambda h: (0, 2 * HEADS + h)),
        pl.BlockSpec((1, PATCHES, 1), lambda h: (h, 0, 0)),
        pl.BlockSpec((1, 1, PATCHES), lambda h: (h, 0, 0)),
    ]


def attend(qkv, gcol, grow):
    return pl.pallas_call(
        attend_kernel,
        grid=(HEADS,),
        out_shape=jax.ShapeDtypeStruct((PATCHES, WIDE), BF16),
        in_specs=head_specs(),
        out_specs=pl.BlockSpec((PATCHES, LANES), lambda h: (0, h)),
        cost_estimate=pl.CostEstimate(
            flops=HEADS * 4 * PATCHES * PATCHES * LANES,
            bytes_accessed=8 * PATCHES * WIDE,
            transcendentals=HEADS * PATCHES * PATCHES,
        ),
        name="attend",
    )(qkv, qkv, qkv, gcol, grow)


def attend_back(qkv, gcol, grow, grads):
    block = pl.BlockSpec((PATCHES, LANES), lambda h: (0, h))
    return pl.pallas_call(
        attend_back_kernel,
        grid=(HEADS,),
        out_shape=[jax.ShapeDtypeStruct((PATCHES, WIDE), F32)] * 3
        + [
            jax.ShapeDtypeStruct((HEADS, PATCHES, 1), F32),
            jax.ShapeDtypeStruct((HEADS, 1, PATCHES), F32),
        ],
        in_specs=head_specs() + [block],
        out_specs=[block, block, block]
        + [
            pl.BlockSpec((1, PATCHES, 1), lambda h: (h, 0, 0)),
            pl.BlockSpec((1, 1, PATCHES), lambda h: (h, 0, 0)),
        ],
        cost_estimate=pl.CostEstimate(
            flops=HEADS * 10 * PATCHES * PATCHES * LANES,
            bytes_accessed=20 * PATCHES * WIDE,
            transcendentals=HEADS * PATCHES * PATCHES,
        ),
        name="attend_back",
    )(qkv, qkv, qkv, gcol, grow, grads)


def pad_heads(source, axis):
    widths = [(0, 0)] * source.ndim
    widths[axis] = (0, LANES - HD)
    return jnp.pad(source, widths)


def pad_cells(grid):
    return jnp.pad(grid, ((1, 1), (1, 1), (0, 0)))


def pick(source, axis, index):
    return lax.dynamic_index_in_dim(source, index, axis, keepdims=False)


def gather_tokens(source):
    return lax.all_gather(source, "pos", axis=0, tiled=True)


def scatter_tokens(partial):
    pieces = partial.astype(BF16).reshape(TEAM, TOK_DEV, D)
    arrived = lax.all_to_all(pieces, "pos", split_axis=0, concat_axis=0, tiled=True)
    return jnp.sum(arrived.astype(F32), axis=0)


def on_device(
    groups,
    patches,
    condition,
    lengths,
    modulator,
    baseline,
    projector,
    forgetter,
    retention,
    smoother,
    pedestal,
    combiner,
    displacement,
    expander,
    thresholds,
    reducer,
    leveling,
    cotangent,
):
    rows_axes = ("grp", "pos")
    half = lax.axis_index("items")
    halves = lax.axis_size("items")
    group = lax.axis_index("grp")
    place = lax.axis_index("pos")
    devices = groups * TEAM
    depth = D // devices
    inner = FF // devices
    columns = 6 * D // devices
    whole_heads = depth == HD
    upstream = cotangent.astype(F32).reshape(TOK_DEV, D)
    inputs = patches.astype(F32).reshape(TOK_DEV, D)

    condition_float = condition.astype(F32)
    squashed = jax.nn.silu(condition_float).astype(BF16)
    modulation_piece = (dot(squashed, modulator) + baseline).astype(BF16).T
    modulation_all = lax.all_gather(modulation_piece, rows_axes, axis=0, tiled=True)
    modulation = pick(modulation_all, 1, group).astype(F32)
    shift_one, scale_one, gate_one, shift_two, scale_two, gate_two = [
        modulation[part * D : (part + 1) * D] for part in range(6)
    ]

    project_cut = jnp.concatenate(
        [
            projector.reshape(depth, 3, HEADS, TEAM, HD)
            .transpose(3, 0, 1, 2, 4)
            .reshape(TEAM, depth, 3 * HEADS * HD),
            forgetter.reshape(depth, HEADS, TEAM).transpose(2, 0, 1),
        ],
        axis=2,
    )
    project_part = lax.all_to_all(project_cut, "pos", split_axis=0, concat_axis=0, tiled=True)
    project_mine = lax.all_gather(project_part, "grp", axis=0, tiled=True).reshape(D, -1)
    project_wide = jnp.concatenate(
        [
            pad_heads(project_mine[:, : 3 * HEADS * HD].reshape(D, 3 * HEADS, HD), 2).reshape(
                D, 3 * WIDE
            ),
            jnp.pad(project_mine[:, 3 * HEADS * HD :], ((0, 0), (0, LANES - HEADS))),
        ],
        axis=1,
    )
    expand_cut = (
        expander.reshape(depth, groups, TEAM, inner)
        .transpose(2, 0, 1, 3)
        .reshape(TEAM, depth, groups * inner)
    )
    expand_part = lax.all_to_all(expand_cut, "pos", split_axis=0, concat_axis=0, tiled=True)
    expand_mine = lax.all_gather(expand_part, "grp", axis=0, tiled=True).reshape(D, groups * inner)
    reduce_mine = lax.all_gather(reducer, "grp", axis=0, tiled=True)
    if whole_heads:
        combine_mine = lax.all_gather(combiner, "grp", axis=0, tiled=True).reshape(HEADS, HD, D)
    else:
        combine_all = lax.all_gather(combiner, rows_axes, axis=0, tiled=True)
        combine_mine = pick(combine_all.reshape(HEADS, TEAM, HD, D), 1, place)
    combine_wide = pad_heads(combine_mine, 1).reshape(WIDE, D)
    thresholds_mine = pick(thresholds.reshape(groups, TEAM, inner), 1, place).reshape(-1)
    retention_mine = pick(retention.reshape(HEADS, TEAM), 1, place)
    kernel = pad_heads(pick(smoother.reshape(9, HEADS, TEAM, HD), 2, place), 2).reshape(9, WIDE)
    offset = pad_heads(pick(pedestal.reshape(HEADS, TEAM, HD), 1, place), 1).reshape(WIDE)

    hidden = modulate(inputs, shift_one, scale_one).astype(BF16)
    hidden_all = gather_tokens(hidden)
    projected = dot(hidden_all, project_wide)
    forget_logit = projected[:, 3 * WIDE : 3 * WIDE + HEADS] + retention_mine
    decays = (jax.nn.log_sigmoid(forget_logit) / 16.0).astype(BF16)
    index = jnp.arange(PATCHES, dtype=jnp.int32)
    length = pick(lengths, 0, group)
    validity = (index < length)[:, None]
    is_query = jnp.arange(3 * WIDE) < WIDE
    keep = validity | is_query[None, :]
    qkv = jnp.where(keep, projected[:, : 3 * WIDE], 0.0).astype(BF16)
    order = column_place(index)
    causal = (order[None, :] <= order[:, None]).astype(BF16)
    summed = dot(causal, decays)
    gcol = summed.T[:, :, None]
    grow = summed.T[:, None, :]
    attended = attend(qkv, gcol, grow)

    attended_grid = attended.astype(F32).reshape(GRID, GRID, WIDE)
    attended_padded = pad_cells(attended_grid)
    smoothed = jnp.zeros_like(attended_grid) + offset
    for tap in range(9):
        down, right = tap // 3, tap % 3
        smoothed = (
            smoothed + kernel[tap] * attended_padded[down : down + GRID, right : right + GRID]
        )
    smoothed = smoothed.astype(BF16).reshape(PATCHES, WIDE)
    branch = scatter_tokens(dot(smoothed, combine_wide)) + displacement
    middle = inputs + gate_one * branch
    hidden_two = modulate(middle, shift_two, scale_two).astype(BF16)
    hidden_two_all = gather_tokens(hidden_two)
    expanded = dot(hidden_two_all, expand_mine) + thresholds_mine
    activated = jax.nn.gelu(expanded, approximate=True).astype(BF16)
    reduced = scatter_tokens(dot(activated, reduce_mine)) + leveling
    block_output = (middle + gate_two * reduced).astype(BF16).reshape(ROWS_DEV, GRID, D)

    gate_two_grad = jnp.sum(upstream * reduced, axis=0)
    reduced_grad = (gate_two * upstream).astype(BF16)
    leveling_grad = jnp.sum(reduced_grad.astype(F32), axis=0)
    reduced_grad_all = gather_tokens(reduced_grad)
    reducer_grad = outer_sum(activated, reduced_grad_all)
    activated_grad = back_dot(reduced_grad_all, reduce_mine)
    pull = jax.vjp(lambda v: jax.nn.gelu(v, approximate=True), expanded)[1]
    expanded_grad = pull(activated_grad)[0].astype(BF16)
    thresholds_grad = jnp.sum(expanded_grad.astype(F32), axis=0)
    expander_grad = outer_sum(hidden_two_all, expanded_grad)
    hidden_two_grad = scatter_tokens(back_dot(expanded_grad, expand_mine))
    second_pull = jax.vjp(modulate, middle, shift_two, scale_two)[1]
    middle_part, shift_two_grad, scale_two_grad = second_pull(hidden_two_grad)
    middle_grad = upstream + middle_part
    gate_one_grad = jnp.sum(middle_grad * branch, axis=0)
    branch_grad = (gate_one * middle_grad).astype(BF16)
    displacement_grad = jnp.sum(branch_grad.astype(F32), axis=0)
    branch_grad_all = gather_tokens(branch_grad)
    combiner_grad = outer_sum(smoothed, branch_grad_all)
    smoothed_grad = back_dot(branch_grad_all, combine_wide).astype(BF16).astype(F32)
    pedestal_grad = jnp.sum(smoothed_grad, axis=0)
    grad_grid = smoothed_grad.reshape(GRID, GRID, WIDE)
    grad_padded = pad_cells(grad_grid)
    tap_grads = []
    attended_grad = jnp.zeros_like(grad_grid)
    for tap in range(9):
        down, right = tap // 3, tap % 3
        tap_grads.append(
            jnp.sum(
                grad_grid * attended_padded[down : down + GRID, right : right + GRID], axis=(0, 1)
            )
        )
        attended_grad = (
            attended_grad
            + kernel[tap] * grad_padded[2 - down : 2 - down + GRID, 2 - right : 2 - right + GRID]
        )
    tap_stack = jnp.stack(tap_grads)
    attended_grad = attended_grad.astype(BF16).reshape(PATCHES, WIDE)
    dq, dk, dv, row_sum, col_sum = attend_back(qkv, gcol, grow, attended_grad)
    moment = row_sum[:, :, 0] - col_sum[:, 0, :]
    decay_grad = lax.dot_general(
        causal.astype(F32),
        moment,
        (((0,), (1,)), ((), ())),
        precision=HIGH,
        preferred_element_type=F32,
    )
    forget_grad = (decay_grad * jax.nn.sigmoid(-forget_logit) / 16.0).astype(BF16)
    retention_grad = jnp.sum(forget_grad.astype(F32), axis=0)
    project_grad = jnp.concatenate(
        [
            dq.astype(BF16),
            jnp.where(validity, dk, 0.0).astype(BF16),
            jnp.where(validity, dv, 0.0).astype(BF16),
            jnp.pad(forget_grad, ((0, 0), (0, LANES - HEADS))),
        ],
        axis=1,
    )
    projector_grad = outer_sum(hidden_all, project_grad)
    hidden_grad = scatter_tokens(back_dot(project_grad, project_wide))
    first_pull = jax.vjp(modulate, inputs, shift_one, scale_one)[1]
    inputs_part, shift_one_grad, scale_one_grad = first_pull(hidden_grad)
    patches_grad = (middle_grad + inputs_part).astype(BF16).reshape(ROWS_DEV, GRID, D)

    def swap_add(share):
        low = share.astype(BF16)
        other = lax.ppermute(low, "items", [(i, (i + 1) % 2) for i in range(2)])
        return low.astype(F32) + other.astype(F32)

    def to_owners(source):
        pieces = source.reshape(devices, depth, source.shape[1])
        arrived = lax.all_to_all(pieces, rows_axes, split_axis=0, concat_axis=0, tiled=True)
        arrived = arrived.reshape(groups, TEAM, depth, source.shape[1])
        return swap_add(jnp.sum(arrived.astype(F32), axis=0))

    expander_share = to_owners(expander_grad.astype(BF16))
    expander_out = (
        expander_share.reshape(TEAM, depth, groups, inner).transpose(1, 2, 0, 3).reshape(depth, FF)
    )
    reducer_pieces = lax.all_to_all(
        reducer_grad.astype(BF16).reshape(groups, inner, D),
        "grp",
        split_axis=0,
        concat_axis=0,
        tiled=True,
    )
    reducer_out = swap_add(jnp.sum(reducer_pieces.astype(F32), axis=0))
    combiner_low = combiner_grad.reshape(HEADS, LANES, D)[:, :HD].astype(BF16)
    if whole_heads:
        combiner_pieces = lax.all_to_all(
            combiner_low, "grp", split_axis=0, concat_axis=0, tiled=True
        )
        combiner_share = jnp.sum(combiner_pieces.astype(F32), axis=0)
    else:
        placed = jnp.zeros((HEADS, TEAM, HD, D), F32)
        placed = lax.dynamic_update_slice_in_dim(
            placed, combiner_low.astype(F32)[:, None], place, 1
        )
        combiner_share = lax.psum_scatter(
            placed.reshape(D, D), rows_axes, scatter_dimension=0, tiled=True
        )
    combiner_out = swap_add(combiner_share)
    projector_low = projector_grad.astype(BF16)
    project_share = to_owners(
        jnp.concatenate(
            [
                projector_low[:, : 3 * WIDE].reshape(D, 3 * HEADS, LANES)[:, :, :HD].reshape(
                    D, 3 * HEADS * HD
                ),
                projector_low[:, 3 * WIDE : 3 * WIDE + HEADS],
            ],
            axis=1,
        )
    )
    projector_out = (
        project_share[:, :, : 3 * HEADS * HD]
        .reshape(TEAM, depth, 3, HEADS, HD)
        .transpose(1, 2, 3, 0, 4)
        .reshape(depth, 3 * D)
    )
    forgetter_out = project_share[:, :, 3 * HEADS * HD :].transpose(1, 2, 0).reshape(depth, H)

    modulation_grad = jnp.concatenate(
        [
            shift_one_grad,
            scale_one_grad,
            gate_one_grad,
            shift_two_grad,
            scale_two_grad,
            gate_two_grad,
        ]
    ).reshape(devices, columns)
    modulation_rows = jnp.sum(
        lax.all_to_all(
            modulation_grad, rows_axes, split_axis=0, concat_axis=0, tiled=True
        ).reshape(groups, TEAM, columns),
        axis=1,
    )
    rows_every = lax.all_gather(modulation_rows, "items", axis=0, tiled=True)
    squashed_every = lax.all_gather(squashed, "items", axis=0, tiled=True).astype(F32)
    modulator_out = lax.dot_general(
        squashed_every, rows_every, (((0,), (0,)), ((), ())), precision=HIGH
    )
    baseline_out = jnp.sum(rows_every, axis=0)
    squashed_grad = jnp.dot(modulation_rows, modulator.astype(F32).T, precision=HIGH)

    def spot(value, shape, axis, at):
        return lax.dynamic_update_slice_in_dim(
            jnp.zeros(shape, F32), jnp.expand_dims(value, axis), at, axis
        ).reshape(-1)

    parts = [
        spot(squashed_grad, (halves, groups, D), 0, half),
        spot(retention_grad, (HEADS, TEAM), 1, place),
        spot(
            tap_stack.reshape(9, HEADS, LANES)[:, :, :HD], (9, HEADS, TEAM, HD), 2, place
        ),
        spot(pedestal_grad.reshape(HEADS, LANES)[:, :HD], (HEADS, TEAM, HD), 1, place),
        displacement_grad,
        spot(thresholds_grad.reshape(groups, inner), (groups, TEAM, inner), 1, place),
        leveling_grad,
    ]
    total = lax.psum(jnp.concatenate(parts), ("items", "grp", "pos"))
    split = []
    start = 0
    for part in parts:
        split.append(total[start : start + part.shape[0]])
        start += part.shape[0]
    squashed_sum = pick(split[0].reshape(halves, groups, D), 0, half)
    silu_pull = jax.vjp(jax.nn.silu, condition_float)[1]
    condition_grad = silu_pull(squashed_sum)[0]
    return (
        block_output,
        patches_grad,
        condition_grad,
        modulator_out,
        baseline_out,
        projector_out,
        forgetter_out,
        split[1],
        split[2].reshape(9, D),
        split[3],
        combiner_out,
        split[4],
        expander_out,
        split[5],
        reducer_out,
        split[6],
    )


def solution(mesh):
    rows = mesh.shape["rows"]
    groups = rows // TEAM
    fine = Mesh(
        mesh.devices.reshape(mesh.shape["items"], groups, TEAM), ("items", "grp", "pos")
    )
    line = ("grp", "pos")
    tokens = P(("items", "grp", "pos"), None, None)
    in_specs = (
        tokens,
        P("items", None),
        P("items"),
        P(None, line),
        P(line),
        P(line, None),
        P(line, None),
        P(),
        P(),
        P(),
        P(line, None),
        P(),
        P(line, None),
        P(),
        P(line, None),
        P(),
        tokens,
    )
    out_specs = (
        tokens,
        tokens,
        P("items", None),
        P(None, line),
        P(line),
        P(line, None),
        P(line, None),
        P(),
        P(),
        P(),
        P(line, None),
        P(),
        P(line, None),
        P(),
        P(line, None),
        P(),
    )
    return jax.shard_map(
        functools.partial(on_device, groups),
        mesh=fine,
        in_specs=in_specs,
        out_specs=out_specs,
        check_vma=False,
    )
```

time: 1430 us -> 715 us (0.50)
  waiting for transfers between devices: 901 us -> 340 us
  matrix products: 186 us -> 64.3 us
  other arithmetic: 92.5 us -> 52.7 us
  blocking collectives: 114 us -> 75.1 us
  starting transfers between devices: 31.9 us -> 61.1 us
  Pallas kernels: 0 us -> 18.2 us
    reduce_scatter x2 -> x0, waiting for transfers between devices: 429 us -> none  [the longest x1 215 us: on_device(): lax.psum_scatter(expander_grad, 'rows', scatter_dimension=0, tiled=True)]
    unnamed x13 -> x7, waiting for transfers between devices: 282 us -> 1.12 us
    dot_general x232 -> x9, matrix products: 130 us -> 28.4 us  [the longest x6 20.8 us: dot(): return jnp.dot(left, right, preferred_element_type=F32)]
    psum x1, waiting for transfers between devices: 5 us -> 107 us  [on_device(): total = lax.psum(jnp.concatenate(parts), ('items', 'grp', 'pos'))]
    psum x2 -> x0, blocking collectives: 72.5 us -> none  [the longest x1 62 us: on_device(): lax.psum((squashed_grad, retention_grad, smoother_grad, pedestal_grad, di...]
    all_to_all x6 -> x11, waiting for transfers between devices: 68.7 us -> 135 us  [the longest x4 90.8 us: scatter_tokens(): lax.all_to_all(pieces, 'pos', split_axis=0, concat_axis=0, tiled=True)]
    all_gather x4 -> x6, waiting for transfers between devices: 116 us -> 79.8 us  [the longest x4 44.3 us: gather_tokens(): return lax.all_gather(source, 'pos', axis=0, tiled=True)]
    all_gather x2 -> x5, blocking collectives: 41.7 us -> 75.1 us  [the longest x1 31.4 us: on_device(): lax.all_gather(project_part, 'grp', axis=0, tiled=True).reshape(D, -1)]
  transfers between devices with their start and end apart: 16 -> 22, of which waited for: 14 -> 12; matrix products, arithmetic and copies ran while one was open for 11% -> 22% of each run, Pallas kernels for 0% -> 3%
where the time goes in v1:
time: 715 us; the launch traced here: 707 us
  waiting for transfers between devices  340 us (48%)
  local copies, waits for them, and re-layouts  79.1 us (11%)
  blocking collectives  75.1 us (11%)
  matrix products  64.3 us (9%)
  starting transfers between devices  61.1 us (9%)
  other arithmetic  52.7 us (7%)
  Pallas kernels  18.2 us (3%)
  between operations  16.6 us (2%)
    psum x1, waiting for transfers between devices, on_device(): total = lax.psum(jnp.concatenate(parts), ('items', 'grp', 'pos'))  107 us
    all_to_all x4, waiting for transfers between devices, scatter_tokens(): lax.all_to_all(pieces, 'pos', split_axis=0, concat_axis=0, tiled=True)  90.8 us
    all_gather x4, waiting for transfers between devices, gather_tokens(): return lax.all_gather(source, 'pos', axis=0, tiled=True)  44.3 us
    all_gather x1, waiting for transfers between devices, on_device(): reduce_mine = lax.all_gather(reducer, 'grp', axis=0, tiled=True)  35.5 us
    all_gather x1, blocking collectives, on_device(): lax.all_gather(project_part, 'grp', axis=0, tiled=True).reshape(D, -1)  31.4 us
    all_to_all x1, waiting for transfers between devices, on_device(): lax.all_to_all(reducer_grad.astype(BF16).reshape(groups, inner, D), 'grp'...  24.2 us
    all_gather x1, blocking collectives, on_device(): lax.all_gather(modulation_piece, rows_axes, axis=0, tiled=True)  23.2 us
    dot_general x6, matrix products, dot(): return jnp.dot(left, right, preferred_element_type=F32)  20.8 us
  transfers between devices with their start and end apart: 22, of which 12 were waited for; matrix products, arithmetic and copies ran while one was open for 22% of the time, Pallas kernels for 3%

profile of v1, /device:TPU:0, one launch (start us, length us, event | category | flops | bytes accessed | tf_op | source)
XLA Modules:
  0.0 707.1 jit_solution(13340892989843994777)
XLA Ops:
  11.6 23.2 %all-gather = bf16[16,432,2]{1,2,0:T(2,128)(2,1)S(1)} all-gather(bf16[1,432,2]{1,2,0:T(2,128)(2,1)S(1)} %fusion.27), channel_id=1, replica_groups=mesh['items'=2,'grp'=2,'pos'=8] {'grp','pos'}, dimensions={0}, use_global_device_ids=true | all-gather | bytes 29376 | tf_op jit(solution)/shard_map/all_gather | solution.py:219
  41.1 3.5 all-to-all-start
  45.5 2.4 reshape.674
  50.3 11.9 %all_gather.36 = bf16[144,1152]{1,0:T(8,128)(2,1)S(1)} all-gather(bf16[72,1152]{1,0:T(8,128)(2,1)} %param.27), channel_id=1, replica_groups=mesh['items'=2,'grp'=2,'pos'=8] {'grp'}, dimensions={0}, use_global_device_ids=true | all-gather | bytes 497664 | tf_op jit(solution)/shard_map/all_gather | solution.py:254
  64.6 4.2 all-to-all-start.2
  68.9 31.4 %all_gather.35 = bf16[16,72,434]{2,1,0:T(8,128)(2,1)S(1)} all-gather(bf16[8,72,434]{2,1,0:T(8,128)(2,1)} %copy-done.15), channel_id=1, replica_groups=mesh['items'=2,'grp'=2,'pos'=8] {'grp'}, dimensions={0}, use_global_device_ids=true | all-gather | bytes 1499904 | tf_op jit(solution)/shard_map/all_gather | solution.py:235
  101.9 2.7 pad.33
  104.7 5.0 fusion.46
  114.7 3.5 fusion.4.q_ref.k_ref.v_ref
  118.1 6.2 attend.1
  127.5 2.3 convolution_convert_fusion.3
  129.8 4.4 all-to-all-start.1
  134.9 42.9 %all-to-all-done.1 = bf16[8,128,1152]{2,1,0:T(8,128)(2,1)} async-done(((bf16[8,128,1152]{2,1,0:T(8,128)(2,1)}), bf16[8,128,1152]{2,1,0:T(8,128)(2,1)}, u32[]{:S(2)}, u32[]{:S(2)}) %all-to-all-start.1) | async-done | bytes 2359328 | tf_op jit(solution)/shard_map/all_to_all | solution.py:179
  183.2 20.9 %all-gather.12.cloned.1.call-done = bf16[1024,1152]{1,0:T(8,128)(2,1)} async-done(((bf16[128,1152]{1,0:T(8,128)(2,1)}), bf16[1024,1152]{1,0:T(8,128)(2,1)}) %all-gather.12.cloned.1.call-update) | async-done | bytes 2359312 | tf_op jit(solution)/shard_map/all_gather | solution.py:174
  204.0 5.3 fusion.105
  209.3 35.5 %all-gather.16.cloned.1.call-done = bf16[576,1152]{1,0:T(8,128)(2,1)} async-done(((bf16[288,1152]{1,0:T(8,128)(2,1)}), bf16[576,1152]{1,0:T(8,128)(2,1)}) %all-gather.16.cloned.1.call-update) | async-done | bytes 1327120 | tf_op jit(solution)/shard_map/all_gather | solution.py:252
  244.8 23.4 %all-gather.18.cloned.1.call-done = bf16[1024,1152]{1,0:T(8,128)(2,1)} async-done(((bf16[128,1152]{1,0:T(8,128)(2,1)}), bf16[1024,1152]{1,0:T(8,128)(2,1)}) %all-gather.18.cloned.1.call-update) | async-done | bytes 2359312 | tf_op jit(solution)/shard_map/all_gather | solution.py:174
  268.2 5.8 convert_reduce_fusion.6
  274.1 3.6 convolution_convert_fusion.1
  277.7 4.4 all-to-all-start.4
  282.1 6.0 convolution_convert_fusion.2
  288.2 22.5 %all-to-all-done.4 = bf16[8,128,1152]{2,1,0:T(8,128)(2,1)} async-done(((bf16[8,128,1152]{2,1,0:T(8,128)(2,1)}), bf16[8,128,1152]{2,1,0:T(8,128)(2,1)}, u32[]{:S(2)}, u32[]{:S(2)}) %all-to-all-start.4) | async-done | bytes 2359328 | tf_op jit(solution)/shard_map/all_to_all | solution.py:179
  310.7 4.4 all-to-all-start.3
  315.3 2.5 convert_reduce_fusion.2
  318.2 25.4 %all-to-all-done.3 = bf16[8,128,1152]{2,1,0:T(8,128)(2,1)} async-done(((bf16[8,128,1152]{2,1,0:T(8,128)(2,1)}), bf16[8,128,1152]{2,1,0:T(8,128)(2,1)}, u32[]{:S(2)}, u32[]{:S(2)}) %all-to-all-start.3) | async-done | bytes 2359328 | tf_op jit(solution)/shard_map/all_to_all | solution.py:179
  343.6 2.1 convert_reduce_fusion.4
  349.2 5.7 convolution_convert_fusion.6
  354.9 3.8 all-to-all-start.10
  358.7 4.8 convolution_convert_fusion.5
  363.4 2.6 copy.176
  366.1 24.2 %all-to-all-done.10 = bf16[2,288,1152]{2,1,0:T(8,128)(2,1)S(1)} async-done(((bf16[2,288,1152]{2,1,0:T(8,128)(2,1)}), bf16[2,288,1152]{2,1,0:T(8,128)(2,1)S(1)}, u32[]{:S(2)}, u32[]{:S(2)}) %all-to-all-start.10) | async-done | bytes 1327136 | tf_op jit(solution)/shard_map/all_to_all | solution.py:379
  391.3 4.0 all-to-all-start.9
  397.3 2.8 fusion.12
  400.9 2.1 multiply_reduce_fusion
  405.6 12.0 %attend_back.1 = (f32[1024,256]{1,0:T(8,128)}, f32[1024,256]{1,0:T(8,128)}, f32[1024,256]{1,0:T(8,128)}, f32[2,1024,1]{2,1,0:T(8,128)}, f32[2,1,1024]{2,1,0:T(1,128)}) custom-call(bf16[1024,768]{1,0:T(8,128)(2,1)} %fusion.4.q_ref.k_ref.v_ref, bf16[1024,768]{1,0:T(8,128)(2,1)} %fusion.4.q_ref.k_ref.v_ref, bf16[1024,768]{1,0:T(8,128)(2,1)} %fusion.4.q_ref.k_ref.v_ref, ...), custom_call_target="tpu_custom_call" | custom-call | flops 2684354560 | bytes 5242880 | tf_op jit(solution)/shard_map/attend_back/pallas_call | solution.py:136
  417.6 2.1 convert_element_type.214
  421.3 4.9 convert_reduce_fusion.10
  427.4 6.6 all-to-all-start.8
  434.0 4.7 convolution_convert_fusion.4
  441.1 5.1 concatenate.29
  446.3 3.0 pad_maximum_fusion
  449.3 3.1 copy.172
  452.4 6.2 all-to-all-start.7
  458.6 2.6 reduce_sum.454
  462.6 6.3 convolution_convert_fusion
  468.9 14.8 %all-to-all-done.7 = bf16[16,72,434]{2,1,0:T(8,128)(2,1)} async-done(((bf16[16,72,434]{2,1,0:T(8,128)(2,1)}), bf16[16,72,434]{2,1,0:T(8,128)(2,1)}, u32[]{:S(2)}, u32[]{:S(2)}) %all-to-all-start.7) | async-done | bytes 999968 | tf_op jit(solution)/shard_map/all_to_all | solution.py:371
  483.7 6.5 all-to-all-start.5
  493.5 2.6 convert_add_fusion.1
  496.1 14.8 %collective-permute-done.2 = bf16[8,72,576]{2,1,0:T(8,128)(2,1)} collective-permute-done((bf16[8,72,576]{2,1,0:T(8,128)(2,1)}, bf16[8,72,576]{2,1,0:T(8,128)(2,1)}, u32[]{:S(2)}, u32[]{:S(2)}) %collective-permute-start.2) | collective-permute-done | bytes 663584 | tf_op jit(solution)/shard_map/ppermute | solution.py:366
  512.2 2.5 reshape.700
  514.7 3.3 copy.177
  518.0 3.1 reshape.701
  529.5 2.6 collective-permute-done.1
  532.9 2.5 reduce_sum.451
  537.0 2.5 convert_reduce_fusion
  550.8 6.5 all-to-all-start.6
  558.8 5.2 all-to-all-done.6
  565.4 2.7 reshape.694
  568.1 3.3 copy.173
  571.4 3.0 reshape.695
  575.1 4.3 all-gather.2
  580.0 106.7 %all-reduce.10.cloned.1.call-done = f32[23056]{0:T(1024)} async-done(((f32[23056]{0:T(1024)}), f32[23056]{0:T(1024)}) %all-reduce.10.cloned.1.call-update) | async-done | bytes 92240 | tf_op jit(solution)/shard_map/psum | solution.py:462
  688.8 4.4 all-gather.1
  694.7 2.3 fusion.106
  (257 shorter events, 85.6 us)
Async XLA Ops:
  8.0 2.6 copy-start
  8.0 29.1 %copy-start.22 = (bf16[72,3456]{1,0:T(8,128)(2,1)S(1)}, bf16[72,3456]{1,0:T(8,128)(2,1)}, u32[]{:S(2)}) copy-start(bf16[72,3456]{1,0:T(8,128)(2,1)} %param.22) | copy-start | bytes 1492996
  8.0 96.6 %all-gather.10.cloned.1.call-start = ((), (), s32[]{:S(2)}) async-start(), calls=%async_computation.11 | async-start | bytes 2654208 | tf_op jit(solution)/shard_map/all_gather | solution.py:174
  10.5 29.0 %copy-start.28 = (f32[4,32]{1,0:T(4,128)}, f32[4,32]{1,0:T(4,128)S(1)}, u32[]{:S(2)}) copy-start(f32[4,32]{1,0:T(4,128)S(1)} %fusion.59) | copy-start | bytes 1540
  37.2 2.8 copy-start.35
  39.5 5.2 copy-start.45
  39.5 5.3 copy-start.46
  39.5 5.8 copy-start.24
  39.5 5.9 copy-start.32
  41.1 22.7 %all-to-all-start = ((bf16[8,72,434]{2,1,0:T(8,128)(2,1)}), bf16[8,72,434]{2,1,0:T(8,128)(2,1)S(1)}, u32[]{:S(2)}, u32[]{:S(2)}) async-start(bf16[8,72,434]{2,1,0:T(8,128)(2,1)} %pad_maximum_fusion.1), calls=%async_computation | async-start | bytes 1179648 | tf_op jit(solution)/shard_map/all_to_all | solution.py:234
  50.3 59.4 %copy-start.41 = (f32[2]{0:T(128)}, f32[2]{0:T(128)S(1)}, u32[]{:S(2)}) copy-start(f32[2]{0:T(128)S(1)} %fusion.85) | copy-start | bytes 28
  63.7 51.0 %copy-start.33 = (pred[1024]{0:T(1024)(128)(4,1)}, pred[1024]{0:T(1024)(128)(4,1)S(1)}, u32[]{:S(2)}) copy-start(pred[1024]{0:T(1024)(128)(4,1)S(1)} %iota_compare_fusion.3) | copy-start | bytes 3076
  63.8 45.9 %copy-start.36 = (s32[1024]{0:T(1024)}, s32[1024]{0:T(1024)S(1)}, u32[]{:S(2)}) copy-start(s32[1024]{0:T(1024)S(1)} %fusion.83) | copy-start | bytes 12292
  64.6 65.2 %all-to-all-start.2 = ((bf16[8,72,576]{2,1,0:T(8,128)(2,1)}), bf16[8,72,576]{2,1,0:T(8,128)(2,1)}, u32[]{:S(2)}, u32[]{:S(2)}) async-start(bf16[8,72,576]{2,1,0:T(8,128)(2,1)} %reshape.675), calls=%async_computation.2 | async-start | bytes 1474560 | tf_op jit(solution)/shard_map/all_to_all | solution.py:250
  124.4 3.1 copy-start.16
  129.8 47.9 %all-to-all-start.1 = ((bf16[8,128,1152]{2,1,0:T(8,128)(2,1)}), bf16[8,128,1152]{2,1,0:T(8,128)(2,1)}, u32[]{:S(2)}, u32[]{:S(2)}) async-start(bf16[8,128,1152]{2,1,0:T(8,128)(2,1)} %bitcast.27), calls=%async_computation.1 | async-start | bytes 4718592 | tf_op jit(solution)/shard_map/all_to_all | solution.py:179
  134.2 45.6 %copy-start.1 = (bf16[4,32,1152]{2,1,0:T(8,128)(2,1)S(1)}, bf16[4,32,1152]{2,1,0:T(8,128)(2,1)}, u32[]{:S(2)}) copy-start(bf16[4,32,1152]{2,1,0:T(8,128)(2,1)} %param.17) | copy-start | bytes 884740
  134.2 45.6 %copy-start.23 = (f32[1152]{0:T(1024)S(1)}, f32[1152]{0:T(1024)}, u32[]{:S(2)}) copy-start(f32[1152]{0:T(1024)} %param.28) | copy-start | bytes 13828
  134.2 48.9 %all-gather.14.cloned.1.call-start = ((), (), s32[]{:S(2)}) async-start(), calls=%async_computation.13 | async-start | bytes 2211840 | tf_op jit(solution)/shard_map/all_gather | solution.py:251
  134.8 69.2 %all-gather.12.cloned.1.call-start = ((), (), s32[]{:S(2)}) async-start(), calls=%async_computation.12 | async-start | bytes 2654208 | tf_op jit(solution)/shard_map/all_gather | solution.py:174
  179.8 2.4 copy-start.13
  179.8 3.1 copy-start.26
  181.4 63.4 %all-gather.16.cloned.1.call-start = ((), (), s32[]{:S(2)}) async-start(), calls=%async_computation.14 | async-start | bytes 1990656 | tf_op jit(solution)/shard_map/all_gather | solution.py:252
  182.0 86.3 %all-gather.18.cloned.1.call-start = ((), (), s32[]{:S(2)}) async-start(), calls=%async_computation.15 | async-start | bytes 2654208 | tf_op jit(solution)/shard_map/all_gather | solution.py:174
  268.2 5.9 copy-start.44
  274.1 3.6 copy-start.47
  277.7 32.9 %all-to-all-start.4 = ((bf16[8,128,1152]{2,1,0:T(8,128)(2,1)}), bf16[8,128,1152]{2,1,0:T(8,128)(2,1)}, u32[]{:S(2)}, u32[]{:S(2)}) async-start(bf16[8,128,1152]{2,1,0:T(8,128)(2,1)} %bitcast.208), calls=%async_computation.4 | async-start | bytes 4718592 | tf_op jit(solution)/shard_map/all_to_all | solution.py:179
  310.7 32.9 %all-to-all-start.3 = ((bf16[8,128,1152]{2,1,0:T(8,128)(2,1)}), bf16[8,128,1152]{2,1,0:T(8,128)(2,1)}, u32[]{:S(2)}, u32[]{:S(2)}) async-start(bf16[8,128,1152]{2,1,0:T(8,128)(2,1)} %bitcast.207), calls=%async_computation.3 | async-start | bytes 4718592 | tf_op jit(solution)/shard_map/all_to_all | solution.py:179
  315.1 82.2 %all-gather.20.cloned.1.call-start = ((), (), s32[]{:S(2)}) async-start(), calls=%async_computation.16 | async-start | bytes 2654208 | tf_op jit(solution)/shard_map/all_gather | solution.py:174
  317.8 27.8 %copy-start.25 = (f32[1152]{0:T(1024)S(1)}, f32[1152]{0:T(1024)}, u32[]{:S(2)}) copy-start(f32[1152]{0:T(1024)} %param.32) | copy-start | bytes 13828
  348.0 6.9 copy-start.30
  354.9 35.3 %all-to-all-start.10 = ((bf16[2,288,1152]{2,1,0:T(8,128)(2,1)}), bf16[2,288,1152]{2,1,0:T(8,128)(2,1)S(1)}, u32[]{:S(2)}, u32[]{:S(2)}) async-start(bf16[2,288,1152]{2,1,0:T(8,128)(2,1)} %bitcast.214), calls=%async_computation.10 | async-start | bytes 2654208 | tf_op jit(solution)/shard_map/all_to_all | solution.py:379
  391.3 36.1 %all-to-all-start.9 = ((bf16[16,72,576]{2,1,0:T(8,128)(2,1)}), bf16[16,72,576]{2,1,0:T(8,128)(2,1)S(1)}, u32[]{:S(2)}, u32[]{:S(2)}) async-start(bf16[16,72,576]{2,1,0:T(8,128)(2,1)} %bitcast.197), calls=%async_computation.9 | async-start | bytes 2949120 | tf_op jit(solution)/shard_map/all_to_all | solution.py:371
  397.3 3.6 copy-start.9
  397.3 3.6 copy-start.17
  397.3 3.6 copy-start.43
  417.6 3.7 copy-start.37
  417.6 3.7 copy-start.42
  417.6 3.7 copy-start.48
  421.3 4.9 copy-start.19
  421.3 4.9 copy-start.20
  421.3 4.9 copy-start.34
  427.4 25.0 %all-to-all-start.8 = ((bf16[2,72,1152]{2,1,0:T(8,128)(2,1)}), bf16[2,72,1152]{2,1,0:T(8,128)(2,1)}, u32[]{:S(2)}, u32[]{:S(2)}) async-start(bf16[2,72,1152]{2,1,0:T(8,128)(2,1)} %slice.398), calls=%async_computation.8 | async-start | bytes 663552 | tf_op jit(solution)/shard_map/all_to_all | solution.py:389
  440.1 6.1 slice-start
  452.4 31.3 %all-to-all-start.7 = ((bf16[16,72,434]{2,1,0:T(8,128)(2,1)}), bf16[16,72,434]{2,1,0:T(8,128)(2,1)}, u32[]{:S(2)}, u32[]{:S(2)}) async-start(bf16[16,72,434]{2,1,0:T(8,128)(2,1)} %copy.172), calls=%async_computation.7 | async-start | bytes 2359296 | tf_op jit(solution)/shard_map/all_to_all | solution.py:371
  461.2 32.3 %collective-permute-start.3 = (bf16[288,1152]{1,0:T(8,128)(2,1)}, bf16[288,1152]{1,0:T(8,128)(2,1)}, u32[]{:S(2)}, u32[]{:S(2)}) collective-permute-start(bf16[288,1152]{1,0:T(8,128)(2,1)} %reduce_sum.454), channel_id=1, source_target_pairs={{0,16},{16,0},{1,17},{17,1},{2,18},{18,2},{3,19},{19,3},{4,20},{20... | collective-permute-start | bytes 1990664 | tf_op jit(solution)/shard_map/ppermute | solution.py:366
  483.7 53.2 %all-to-all-start.5 = ((bf16[8,128,1152]{2,1,0:T(8,128)(2,1)}), bf16[8,128,1152]{2,1,0:T(8,128)(2,1)}, u32[]{:S(2)}, u32[]{:S(2)}) async-start(bf16[8,128,1152]{2,1,0:T(8,128)(2,1)} %bitcast.206), calls=%async_computation.5 | async-start | bytes 4718592 | tf_op jit(solution)/shard_map/all_to_all | solution.py:179
  491.6 19.2 %collective-permute-start.2 = (bf16[8,72,576]{2,1,0:T(8,128)(2,1)}, bf16[8,72,576]{2,1,0:T(8,128)(2,1)}, u32[]{:S(2)}, u32[]{:S(2)}) collective-permute-start(bf16[8,72,576]{2,1,0:T(8,128)(2,1)} %reduce_sum.453), channel_id=1, source_target_pairs={{0,16},{16,0},{1,17},{17,1},{2,18},{18,2},{3,19},{19,3},{4,20},{20... | collective-permute-start | bytes 1990664 | tf_op jit(solution)/shard_map/ppermute | solution.py:366
  493.5 17.4 %copy-start.12 = (bf16[8,72,576]{2,1,0:T(8,128)(2,1)S(1)}, bf16[8,72,576]{2,1,0:T(8,128)(2,1)}, u32[]{:S(2)}) copy-start(bf16[8,72,576]{2,1,0:T(8,128)(2,1)} %reduce_sum.453) | copy-start | bytes 1990660
  517.9 3.1 copy-start.6
  517.9 3.1 copy-start.11
  517.9 7.3 %copy-start.39 = (f32[256]{0:T(256)S(1)}, f32[256]{0:T(256)}, u32[]{:S(2)}) copy-start(f32[256]{0:T(256)} %get-tuple-element.36) | copy-start | bytes 3076
  517.9 9.9 %copy-start.38 = (f32[256]{0:T(256)S(1)}, f32[256]{0:T(256)}, u32[]{:S(2)}) copy-start(f32[256]{0:T(256)} %get-tuple-element.30) | copy-start | bytes 3076
  526.3 5.9 collective-permute-start.1
  535.4 4.3 copy-start.29
  535.4 4.7 copy-start.3
  535.4 4.7 copy-start.5
  535.4 4.7 copy-start.14
  535.4 4.7 copy-start.31
  535.4 21.9 %collective-permute-start = (bf16[8,72,434]{2,1,0:T(8,128)(2,1)}, bf16[8,72,434]{2,1,0:T(8,128)(2,1)}, u32[]{:S(2)}, u32[]{:S(2)}) collective-permute-start(bf16[8,72,434]{2,1,0:T(8,128)(2,1)} %reduce_sum.451), channel_id=1, source_target_pairs={{0,16},{16,0},{1,17},{17,1},{2,18},{18,2},{3,19},{19,3},{4,20},{20... | collective-permute-start | bytes 1499912 | tf_op jit(solution)/shard_map/ppermute | solution.py:366
  541.5 23.0 %copy-start.40 = (f32[16]{0:T(128)S(1)}, f32[16]{0:T(128)}, u32[]{:S(2)}) copy-start(f32[16]{0:T(128)} %reshape.686) | copy-start | bytes 196
  550.8 13.1 %all-to-all-start.6 = ((f32[16,1,432]{2,1,0:T(1,128)}), f32[16,1,432]{2,1,0:T(1,128)S(1)}, u32[]{:S(2)}, u32[]{:S(2)}) async-start(f32[16,1,432]{2,1,0:T(1,128)} %all_to_all.42), calls=%async_computation.6 | async-start | bytes 65536 | tf_op jit(solution)/shard_map/all_to_all | solution.py:433
  557.3 129.4 %all-reduce.10.cloned.1.call-start = ((), (), s32[]{:S(2)}) async-start(), calls=%async_computation.17 | async-start | bytes 188416 | tf_op jit(solution)/shard_map/psum | solution.py:462
  571.4 116.8 %copy-start.27 = (bf16[2,1152]{1,0:T(2,128)(2,1)S(1)}, bf16[2,1152]{1,0:T(2,128)(2,1)}, u32[]{:S(2)}) copy-start(bf16[2,1152]{1,0:T(2,128)(2,1)} %param.18) | copy-start | bytes 13828
  (8 other events, 10.6 us)
Sparse Core Ops, SparseCore 0:
  37.3 28.3 all-gather.9
  349.3 29.2 all-gather.19
  565.4 121.2 all-reduce.9
Sparse Core Ops, SparseCore 1:
  136.3 44.1 all-gather.13
  182.5 21.5 all-gather.11
  205.5 39.3 all-gather.15
  247.1 21.1 all-gather.17

commit v2 on v1

--- a/solution.py
+++ b/solution.py
@@ -170,14 +170,311 @@
     return lax.dynamic_index_in_dim(source, index, axis, keepdims=False)
 
 
-def gather_tokens(source):
-    return lax.all_gather(source, "pos", axis=0, tiled=True)
-
-
-def scatter_tokens(partial):
-    pieces = partial.astype(BF16).reshape(TEAM, TOK_DEV, D)
-    arrived = lax.all_to_all(pieces, "pos", split_axis=0, concat_axis=0, tiled=True)
-    return jnp.sum(arrived.astype(F32), axis=0)
+MESH = pl.DeviceIdType.MESH
+
+
+def greet(peers):
+    barrier = pltpu.get_barrier_semaphore()
+    for peer in peers:
+        pl.semaphore_signal(barrier, inc=1, device_id=peer, device_id_type=MESH)
+    pl.semaphore_wait(barrier, len(peers))
+
+
+def team_peers():
+    place = lax.axis_index("pos")
+    up, side, core = place // 4, (place // 2) % 2, place % 2
+    return up, side, core
+
+
+def seat(up, side, core):
+    return up * 4 + side * 2 + core
+
+
+def team_gather_kernel(x_ref, out_ref, send_sem, recv_sem):
+    up, side, core = team_peers()
+    mine = seat(up, side, core)
+    above, beside, across = (
+        seat(1 - up, side, core),
+        seat(up, 1 - side, core),
+        seat(1 - up, 1 - side, core),
+    )
+    twin = {"pos": seat(up, side, 1 - core)}
+    to_up = {"pos": above}
+    to_side = {"pos": beside}
+    greet((to_up, to_side, twin))
+    rows = x_ref.shape[0]
+    parts = (pl.ds(0, rows // 2), pl.ds(rows // 2, rows // 2))
+
+    def send(slot, source, owner, part, peer):
+        copy = pltpu.make_async_remote_copy(
+            src_ref=source,
+            dst_ref=out_ref.at[owner, part],
+            send_sem=send_sem.at[slot],
+            recv_sem=recv_sem.at[slot],
+            device_id=peer,
+            device_id_type=MESH,
+        )
+        copy.start()
+        return copy
+
+    held = [
+        send(0, x_ref.at[parts[0]], mine, parts[0], to_up),
+        send(1, x_ref.at[parts[1]], mine, parts[1], to_side),
+        send(2, x_ref.at[parts[1]], mine, parts[1], to_up),
+        send(3, x_ref.at[parts[0]], mine, parts[0], to_side),
+        send(4, x_ref.at[parts[0]], mine, parts[0], twin),
+        send(5, x_ref.at[parts[1]], mine, parts[1], twin),
+    ]
+    out_ref[mine] = x_ref[...]
+    held[0].wait_recv()
+    held.append(send(6, out_ref.at[above, parts[0]], above, parts[0], to_side))
+    held.append(send(7, out_ref.at[above, parts[0]], above, parts[0], twin))
+    held[1].wait_recv()
+    held.append(send(8, out_ref.at[beside, parts[1]], beside, parts[1], to_up))
+    held.append(send(9, out_ref.at[beside, parts[1]], beside, parts[1], twin))
+    held[2].wait_recv()
+    held.append(send(10, out_ref.at[above, parts[1]], above, parts[1], twin))
+    held[3].wait_recv()
+    held.append(send(11, out_ref.at[beside, parts[0]], beside, parts[0], twin))
+    held[6].wait_recv()
+    held.append(send(12, out_ref.at[across, parts[0]], across, parts[0], twin))
+    held[8].wait_recv()
+    held.append(send(13, out_ref.at[across, parts[1]], across, parts[1], twin))
+    for slot in (4, 5, 7, 9, 10, 11, 12, 13):
+        held[slot].wait_recv()
+    for copy in held:
+        copy.wait_send()
+
+
+def team_gather(source):
+    rows, width = source.shape
+    vmem = pl.BlockSpec(memory_space=pltpu.VMEM)
+    return pl.pallas_call(
+        team_gather_kernel,
+        out_shape=jax.ShapeDtypeStruct((TEAM, rows, width), source.dtype),
+        in_specs=[vmem],
+        out_specs=vmem,
+        scratch_shapes=[pltpu.SemaphoreType.DMA((14,)), pltpu.SemaphoreType.DMA((14,))],
+        compiler_params=pltpu.CompilerParams(collective_id=1, has_side_effects=True),
+        name="team_gather",
+    )(source).reshape(TEAM * rows, width)
+
+
+def team_scatter_kernel(x_ref, out_ref, twins, low, first, turned, second, send_sem, recv_sem):
+    up, side, core = team_peers()
+    twin = {"pos": seat(up, side, 1 - core)}
+    to_up = {"pos": seat(1 - up, side, core)}
+    to_side = {"pos": seat(up, 1 - side, core)}
+    greet((to_up, to_side, twin))
+    rows = x_ref.shape[1]
+    part_rows = rows // 2
+    parts = (pl.ds(0, part_rows), pl.ds(part_rows, part_rows))
+
+    def send(slot, source, target, peer):
+        copy = pltpu.make_async_remote_copy(
+            src_ref=source,
+            dst_ref=target,
+            send_sem=send_sem.at[slot],
+            recv_sem=recv_sem.at[slot],
+            device_id=peer,
+            device_id_type=MESH,
+        )
+        copy.start()
+        return copy
+
+    chips = ((1 - up, 1 - side), (1 - up, side), (up, 1 - side), (up, side))
+    held = []
+    for slot, (u, s) in enumerate(chips):
+        held.append(send(slot, x_ref.at[seat(u, s, 1 - core)], twins.at[u * 2 + s], twin))
+
+    def merge(slot):
+        u, s = chips[slot]
+        held[slot].wait_recv()
+        low[u * 2 + s] = (
+            x_ref[seat(u, s, core)].astype(F32) + twins[u * 2 + s].astype(F32)
+        ).astype(BF16)
+
+    merge(0)
+    a_far = send(4, low.at[(1 - up) * 2 + 1 - side, parts[0]], first.at[1 - side], to_up)
+    b_far = send(5, low.at[(1 - up) * 2 + 1 - side, parts[1]], first.at[2 + 1 - up], to_side)
+    merge(1)
+    a_near = send(6, low.at[(1 - up) * 2 + side, parts[0]], first.at[side], to_up)
+    merge(2)
+    b_near = send(7, low.at[up * 2 + 1 - side, parts[1]], first.at[2 + up], to_side)
+    merge(3)
+    a_far.wait_recv()
+    turned[0] = (
+        low[up * 2 + 1 - side, parts[0]].astype(F32) + first[1 - side].astype(F32)
+    ).astype(BF16)
+    a_last = send(8, turned.at[0], second.at[0], to_side)
+    b_far.wait_recv()
+    turned[1] = (
+        low[(1 - up) * 2 + side, parts[1]].astype(F32) + first[2 + 1 - up].astype(F32)
+    ).astype(BF16)
+    b_last = send(9, turned.at[1], second.at[1], to_up)
+    a_near.wait_recv()
+    b_near.wait_recv()
+    a_last.wait_recv()
+    out_ref[parts[0]] = (
+        low[up * 2 + side, parts[0]].astype(F32)
+        + first[side].astype(F32)
+        + second[0].astype(F32)
+    )
+    b_last.wait_recv()
+    out_ref[parts[1]] = (
+        low[up * 2 + side, parts[1]].astype(F32)
+        + first[2 + up].astype(F32)
+        + second[1].astype(F32)
+    )
+    for copy in held + [a_far, b_far, a_near, b_near, a_last, b_last]:
+        copy.wait_send()
+
+
+def team_scatter(partial):
+    rows, width = partial.shape[0] // TEAM, partial.shape[1]
+    vmem = pl.BlockSpec(memory_space=pltpu.VMEM)
+    return pl.pallas_call(
+        team_scatter_kernel,
+        out_shape=jax.ShapeDtypeStruct((rows, width), F32),
+        in_specs=[vmem],
+        out_specs=vmem,
+        scratch_shapes=[
+            pltpu.VMEM((4, rows, width), BF16),
+            pltpu.VMEM((4, rows, width), BF16),
+            pltpu.VMEM((4, rows // 2, width), BF16),
+            pltpu.VMEM((2, rows // 2, width), BF16),
+            pltpu.VMEM((2, rows // 2, width), BF16),
+            pltpu.SemaphoreType.DMA((10,)),
+            pltpu.SemaphoreType.DMA((10,)),
+        ],
+        compiler_params=pltpu.CompilerParams(collective_id=2, has_side_effects=True),
+        name="team_scatter",
+    )(partial.astype(BF16).reshape(TEAM, rows, width))
+
+
+def flat_peer(index, sizes):
+    halves, groups = sizes
+    where = {"grp": (index // TEAM) % groups, "pos": index % TEAM}
+    if halves > 1:
+        where["items"] = index // (TEAM * groups)
+    return where
+
+
+def flat_index(sizes):
+    halves, groups = sizes
+    here = lax.axis_index("grp") * TEAM + lax.axis_index("pos")
+    if halves > 1:
+        here = here + lax.axis_index("items") * (TEAM * groups)
+    return here
+
+
+def greet_all(me, total, sizes):
+    barrier = pltpu.get_barrier_semaphore()
+
+    def call(step, carry):
+        pl.semaphore_signal(
+            barrier,
+            inc=1,
+            device_id=flat_peer((me + step) % total, sizes),
+            device_id_type=MESH,
+        )
+        return carry
+
+    lax.fori_loop(1, total, call, 0)
+    pl.semaphore_wait(barrier, total - 1)
+
+
+def send_all(me, total, sizes, source_of, target, send_sem, recv_sem, whole):
+    def describe(step):
+        peer = (me + step) % total
+        return pltpu.make_async_remote_copy(
+            src_ref=source_of(peer),
+            dst_ref=target,
+            send_sem=send_sem,
+            recv_sem=recv_sem,
+            device_id=flat_peer(peer, sizes),
+            device_id_type=MESH,
+        )
+
+    def start(step, carry):
+        describe(step).start()
+        return carry
+
+    lax.fori_loop(1, total, start, 0)
+    everything = pltpu.make_async_remote_copy(
+        src_ref=whole.at[pl.ds(0, total - 1)],
+        dst_ref=whole.at[pl.ds(0, total - 1)],
+        send_sem=send_sem,
+        recv_sem=recv_sem,
+        device_id=flat_peer((me + 1) % total, sizes),
+        device_id_type=MESH,
+    )
+    everything.wait_recv()
+    everything.wait_send()
+
+
+def small_gather_kernel(sizes, x_ref, out_ref, send_sem, recv_sem):
+    total = sizes[0] * sizes[1] * TEAM
+    me = flat_index(sizes)
+    greet_all(me, total, sizes)
+    out_ref[me] = x_ref[...]
+    send_all(me, total, sizes, lambda peer: x_ref, out_ref.at[me], send_sem, recv_sem, out_ref)
+
+
+def small_gather(source, sizes, number):
+    total = sizes[0] * sizes[1] * TEAM
+    count = source.shape[0]
+    lines = -(-count // 1024) * 8
+    padded = jnp.pad(source, (0, lines * 128 - count)).reshape(lines, 128)
+    vmem = pl.BlockSpec(memory_space=pltpu.VMEM)
+    out = pl.pallas_call(
+        functools.partial(small_gather_kernel, sizes),
+        out_shape=jax.ShapeDtypeStruct((total, lines, 128), F32),
+        in_specs=[vmem],
+        out_specs=vmem,
+        scratch_shapes=[pltpu.SemaphoreType.DMA, pltpu.SemaphoreType.DMA],
+        compiler_params=pltpu.CompilerParams(collective_id=number, has_side_effects=True),
+        name="small_gather",
+    )(padded)
+    return out.reshape(total, lines * 128)[:, :count]
+
+
+def small_sum_kernel(sizes, x_ref, out_ref, came, summed, sems):
+    total = sizes[0] * sizes[1] * TEAM
+    me = flat_index(sizes)
+    greet_all(me, total, sizes)
+    came[me] = x_ref[me]
+    send_all(
+        me, total, sizes, lambda peer: x_ref.at[peer], came.at[me], sems.at[0], sems.at[1], came
+    )
+    result = jnp.sum(came[...], axis=0)
+    summed[...] = result
+    out_ref[me] = result
+    send_all(
+        me, total, sizes, lambda peer: summed, out_ref.at[me], sems.at[2], sems.at[3], out_ref
+    )
+
+
+def small_sum(source, sizes, number):
+    total = sizes[0] * sizes[1] * TEAM
+    count = source.shape[0]
+    lines = -(-count // (1024 * total)) * 8
+    padded = jnp.pad(source, (0, total * lines * 128 - count)).reshape(total, lines, 128)
+    vmem = pl.BlockSpec(memory_space=pltpu.VMEM)
+    out = pl.pallas_call(
+        functools.partial(small_sum_kernel, sizes),
+        out_shape=jax.ShapeDtypeStruct((total, lines, 128), F32),
+        in_specs=[vmem],
+        out_specs=vmem,
+        scratch_shapes=[
+            pltpu.VMEM((total, lines, 128), F32),
+            pltpu.VMEM((lines, 128), F32),
+            pltpu.SemaphoreType.DMA((4,)),
+        ],
+        compiler_params=pltpu.CompilerParams(collective_id=number, has_side_effects=True),
+        name="small_sum",
+    )(padded)
+    return out.reshape(-1)[:count]
 
 
 def on_device(
@@ -216,11 +513,22 @@
     condition_float = condition.astype(F32)
     squashed = jax.nn.silu(condition_float).astype(BF16)
     modulation_piece = (dot(squashed, modulator) + baseline).astype(BF16).T
-    modulation_all = lax.all_gather(modulation_piece, rows_axes, axis=0, tiled=True)
-    modulation = pick(modulation_all, 1, group).astype(F32)
+    modulation_all = small_gather(
+        modulation_piece.T.astype(F32).reshape(-1), (1, groups), 3
+    ).reshape(devices, groups, columns)
+    modulation = pick(modulation_all, 1, group).reshape(-1)
     shift_one, scale_one, gate_one, shift_two, scale_two, gate_two = [
         modulation[part * D : (part + 1) * D] for part in range(6)
     ]
+
+    def group_gather(source):
+        if groups != 2:
+            return lax.all_gather(source, "grp", axis=0, tiled=True)
+        other = lax.ppermute(source, "grp", [(0, 1), (1, 0)])
+        first = group == 0
+        return jnp.concatenate(
+            [jnp.where(first, source, other), jnp.where(first, other, source)], axis=0
+        )
 
     project_cut = jnp.concatenate(
         [
@@ -232,7 +540,7 @@
         axis=2,
     )
     project_part = lax.all_to_all(project_cut, "pos", split_axis=0, concat_axis=0, tiled=True)
-    project_mine = lax.all_gather(project_part, "grp", axis=0, tiled=True).reshape(D, -1)
+    project_mine = group_gather(project_part).reshape(D, -1)
     project_wide = jnp.concatenate(
         [
             pad_heads(project_mine[:, : 3 * HEADS * HD].reshape(D, 3 * HEADS, HD), 2).reshape(
@@ -248,10 +556,10 @@
         .reshape(TEAM, depth, groups * inner)
     )
     expand_part = lax.all_to_all(expand_cut, "pos", split_axis=0, concat_axis=0, tiled=True)
-    expand_mine = lax.all_gather(expand_part, "grp", axis=0, tiled=True).reshape(D, groups * inner)
-    reduce_mine = lax.all_gather(reducer, "grp", axis=0, tiled=True)
+    expand_mine = group_gather(expand_part).reshape(D, groups * inner)
+    reduce_mine = group_gather(reducer)
     if whole_heads:
-        combine_mine = lax.all_gather(combiner, "grp", axis=0, tiled=True).reshape(HEADS, HD, D)
+        combine_mine = group_gather(combiner).reshape(HEADS, HD, D)
     else:
         combine_all = lax.all_gather(combiner, rows_axes, axis=0, tiled=True)
         combine_mine = pick(combine_all.reshape(HEADS, TEAM, HD, D), 1, place)
@@ -262,7 +570,7 @@
     offset = pad_heads(pick(pedestal.reshape(HEADS, TEAM, HD), 1, place), 1).reshape(WIDE)
 
     hidden = modulate(inputs, shift_one, scale_one).astype(BF16)
-    hidden_all = gather_tokens(hidden)
+    hidden_all = team_gather(hidden)
     projected = dot(hidden_all, project_wide)
     forget_logit = projected[:, 3 * WIDE : 3 * WIDE + HEADS] + retention_mine
     decays = (jax.nn.log_sigmoid(forget_logit) / 16.0).astype(BF16)
@@ -288,33 +596,33 @@
             smoothed + kernel[tap] * attended_padded[down : down + GRID, right : right + GRID]
         )
     smoothed = smoothed.astype(BF16).reshape(PATCHES, WIDE)
-    branch = scatter_tokens(dot(smoothed, combine_wide)) + displacement
+    branch = team_scatter(dot(smoothed, combine_wide)) + displacement
     middle = inputs + gate_one * branch
     hidden_two = modulate(middle, shift_two, scale_two).astype(BF16)
-    hidden_two_all = gather_tokens(hidden_two)
+    hidden_two_all = team_gather(hidden_two)
     expanded = dot(hidden_two_all, expand_mine) + thresholds_mine
     activated = jax.nn.gelu(expanded, approximate=True).astype(BF16)
-    reduced = scatter_tokens(dot(activated, reduce_mine)) + leveling
+    reduced = team_scatter(dot(activated, reduce_mine)) + leveling
     block_output = (middle + gate_two * reduced).astype(BF16).reshape(ROWS_DEV, GRID, D)
 
     gate_two_grad = jnp.sum(upstream * reduced, axis=0)
     reduced_grad = (gate_two * upstream).astype(BF16)
     leveling_grad = jnp.sum(reduced_grad.astype(F32), axis=0)
-    reduced_grad_all = gather_tokens(reduced_grad)
+    reduced_grad_all = team_gather(reduced_grad)
     reducer_grad = outer_sum(activated, reduced_grad_all)
     activated_grad = back_dot(reduced_grad_all, reduce_mine)
     pull = jax.vjp(lambda v: jax.nn.gelu(v, approximate=True), expanded)[1]
     expanded_grad = pull(activated_grad)[0].astype(BF16)
     thresholds_grad = jnp.sum(expanded_grad.astype(F32), axis=0)
     expander_grad = outer_sum(hidden_two_all, expanded_grad)
-    hidden_two_grad = scatter_tokens(back_dot(expanded_grad, expand_mine))
+    hidden_two_grad = team_scatter(back_dot(expanded_grad, expand_mine))
     second_pull = jax.vjp(modulate, middle, shift_two, scale_two)[1]
     middle_part, shift_two_grad, scale_two_grad = second_pull(hidden_two_grad)
     middle_grad = upstream + middle_part
     gate_one_grad = jnp.sum(middle_grad * branch, axis=0)
     branch_grad = (gate_one * middle_grad).astype(BF16)
     displacement_grad = jnp.sum(branch_grad.astype(F32), axis=0)
-    branch_grad_all = gather_tokens(branch_grad)
+    branch_grad_all = team_gather(branch_grad)
     combiner_grad = outer_sum(smoothed, branch_grad_all)
     smoothed_grad = back_dot(branch_grad_all, combine_wide).astype(BF16).astype(F32)
     pedestal_grad = jnp.sum(smoothed_grad, axis=0)
@@ -356,7 +664,7 @@
         axis=1,
     )
     projector_grad = outer_sum(hidden_all, project_grad)
-    hidden_grad = scatter_tokens(back_dot(project_grad, project_wide))
+    hidden_grad = team_scatter(back_dot(project_grad, project_wide))
     first_pull = jax.vjp(modulate, inputs, shift_one, scale_one)[1]
     inputs_part, shift_one_grad, scale_one_grad = first_pull(hidden_grad)
     patches_grad = (middle_grad + inputs_part).astype(BF16).reshape(ROWS_DEV, GRID, D)
@@ -419,6 +727,20 @@
     )
     forgetter_out = project_share[:, :, 3 * HEADS * HD :].transpose(1, 2, 0).reshape(depth, H)
 
+    def spot(value, shape, axis, at):
+        return lax.dynamic_update_slice_in_dim(
+            jnp.zeros(shape, F32), jnp.expand_dims(value, axis), at, axis
+        ).reshape(-1)
+
+    def sum_everywhere(parts, number):
+        total = small_sum(jnp.concatenate(parts), (halves, groups), number)
+        split = []
+        start = 0
+        for part in parts:
+            split.append(total[start : start + part.shape[0]])
+            start += part.shape[0]
+        return split
+
     modulation_grad = jnp.concatenate(
         [
             shift_one_grad,
@@ -428,44 +750,37 @@
             scale_two_grad,
             gate_two_grad,
         ]
-    ).reshape(devices, columns)
-    modulation_rows = jnp.sum(
-        lax.all_to_all(
-            modulation_grad, rows_axes, split_axis=0, concat_axis=0, tiled=True
-        ).reshape(groups, TEAM, columns),
-        axis=1,
-    )
-    rows_every = lax.all_gather(modulation_rows, "items", axis=0, tiled=True)
-    squashed_every = lax.all_gather(squashed, "items", axis=0, tiled=True).astype(F32)
+    )
+    item = half * groups + group
+    here = ((group == 0) & (place == 0)).astype(F32)
+    split = sum_everywhere(
+        [
+            spot(modulation_grad, (halves * groups, 6 * D), 0, item),
+            spot(retention_grad, (HEADS, TEAM), 1, place),
+            spot(
+                tap_stack.reshape(9, HEADS, LANES)[:, :, :HD], (9, HEADS, TEAM, HD), 2, place
+            ),
+            spot(pedestal_grad.reshape(HEADS, LANES)[:, :HD], (HEADS, TEAM, HD), 1, place),
+            displacement_grad,
+            spot(thresholds_grad.reshape(groups, inner), (groups, TEAM, inner), 1, place),
+            leveling_grad,
+            spot(squashed.astype(F32) * here, (halves, groups, D), 0, half),
+        ],
+        4,
+    )
+    device = group * TEAM + place
+    rows_every = pick(split[0].reshape(halves * groups, devices, columns), 1, device)
+    squashed_every = split[7].reshape(halves * groups, D)
     modulator_out = lax.dot_general(
         squashed_every, rows_every, (((0,), (0,)), ((), ())), precision=HIGH
     )
     baseline_out = jnp.sum(rows_every, axis=0)
+    modulation_rows = pick(rows_every.reshape(halves, groups, columns), 0, half)
     squashed_grad = jnp.dot(modulation_rows, modulator.astype(F32).T, precision=HIGH)
-
-    def spot(value, shape, axis, at):
-        return lax.dynamic_update_slice_in_dim(
-            jnp.zeros(shape, F32), jnp.expand_dims(value, axis), at, axis
-        ).reshape(-1)
-
-    parts = [
-        spot(squashed_grad, (halves, groups, D), 0, half),
-        spot(retention_grad, (HEADS, TEAM), 1, place),
-        spot(
-            tap_stack.reshape(9, HEADS, LANES)[:, :, :HD], (9, HEADS, TEAM, HD), 2, place
-        ),
-        spot(pedestal_grad.reshape(HEADS, LANES)[:, :HD], (HEADS, TEAM, HD), 1, place),
-        displacement_grad,
-        spot(thresholds_grad.reshape(groups, inner), (groups, TEAM, inner), 1, place),
-        leveling_grad,
-    ]
-    total = lax.psum(jnp.concatenate(parts), ("items", "grp", "pos"))
-    split = []
-    start = 0
-    for part in parts:
-        split.append(total[start : start + part.shape[0]])
-        start += part.shape[0]
-    squashed_sum = pick(split[0].reshape(halves, groups, D), 0, half)
+    squashed_total = sum_everywhere(
+        [spot(squashed_grad, (halves, groups, D), 0, half)], 5
+    )[0]
+    squashed_sum = pick(squashed_total.reshape(halves, groups, D), 0, half)
     silu_pull = jax.vjp(jax.nn.silu, condition_float)[1]
     condition_grad = silu_pull(squashed_sum)[0]
     return (

time: 715 us -> 574 us (0.80)
  waiting for transfers between devices: 340 us -> 78.5 us
  Pallas kernels: 18.2 us -> 272 us
  blocking collectives: 75.1 us -> 0 us
  starting transfers between devices: 61.1 us -> 37.7 us
  between operations: 16.6 us -> 2.46 us
  local copies, waits for them, and re-layouts: 79.1 us -> 65.8 us
  matrix products: 64.3 us -> 51.3 us
    pallas_call x0 -> x11, Pallas kernels: none -> 254 us  [the longest x4 87.8 us: team_scatter(): pl.pallas_call(team_scatter_kernel, out_shape=jax.ShapeDtypeStruct((rows,...]
    psum x1 -> x0, waiting for transfers between devices: 107 us -> none  [on_device(): total = lax.psum(jnp.concatenate(parts), ('items', 'grp', 'pos'))]
    all_to_all x5 -> x0, waiting for transfers between devices: 95.9 us -> none  [the longest x4 90.8 us: scatter_tokens(): lax.all_to_all(pieces, 'pos', split_axis=0, concat_axis=0, tiled=True)]
    all_gather x6 -> x0, waiting for transfers between devices: 79.8 us -> none  [the longest x4 44.3 us: gather_tokens(): return lax.all_gather(source, 'pos', axis=0, tiled=True)]
    all_gather x5 -> x0, blocking collectives: 75.1 us -> none  [the longest x1 31.4 us: on_device(): lax.all_gather(project_part, 'grp', axis=0, tiled=True).reshape(D, -1)]
    ppermute x0 -> x4, waiting for transfers between devices: none -> 29.7 us  [group_gather(): other = lax.ppermute(source, 'grp', [(0, 1), (1, 0)])]
    all_to_all x5 -> x0, starting transfers between devices: 26.2 us -> none  [the longest x4 19.7 us: scatter_tokens(): lax.all_to_all(pieces, 'pos', split_axis=0, concat_axis=0, tiled=True)]
    all_to_all x2, waiting for transfers between devices: 14.8 us -> 0.01 us  [to_owners(): lax.all_to_all(pieces, rows_axes, split_axis=0, concat_axis=0, tiled=True)]
  transfers between devices with their start and end apart: 22 -> 14, of which waited for: 12 -> 7; matrix products, arithmetic and copies ran while one was open for 22% -> 20% of each run, Pallas kernels for 3% -> 39%
where the time goes in v2:
time: 574 us; the launch traced here: 566 us
  Pallas kernels  272 us (47%)
  waiting for transfers between devices  78.5 us (14%)
  local copies, waits for them, and re-layouts  65.8 us (11%)
  other arithmetic  57.8 us (10%)
  matrix products  51.3 us (9%)
  starting transfers between devices  37.7 us (7%)
    pallas_call x4, Pallas kernels, team_scatter(): pl.pallas_call(team_scatter_kernel, out_shape=jax.ShapeDtypeStruct((rows,...  87.8 us
    pallas_call x4, Pallas kernels, team_gather(): pl.pallas_call(team_gather_kernel, out_shape=jax.ShapeDtypeStruct((TEAM,...  64.3 us
    pallas_call x2, Pallas kernels, small_sum(): pl.pallas_call(functools.partial(small_sum_kernel, sizes), out_shape=jax....  63.4 us
    pallas_call x1, Pallas kernels, small_gather(): pl.pallas_call(functools.partial(small_gather_kernel, sizes), out_shape=j...  38 us
    ppermute x4, waiting for transfers between devices, group_gather(): other = lax.ppermute(source, 'grp', [(0, 1), (1, 0)])  29.7 us
    ppermute x4, waiting for transfers between devices, swap_add(): other = lax.ppermute(low, 'items', [(i, (i + 1) % 2) for i in range(2)])  24.2 us
    dot_general x4, matrix products, back_dot(): lax.dot_general(gradient, matrix, (((1,), (1,)), ((), ())), preferred_ele...  15.4 us
    dot_general x6, matrix products, dot(): return jnp.dot(left, right, preferred_element_type=F32)  15.1 us
  transfers between devices with their start and end apart: 14, of which 7 were waited for; matrix products, arithmetic and copies ran while one was open for 20% of the time, Pallas kernels for 39%

profile of v2, /device:TPU:0, one launch (start us, length us, event | category | flops | bytes accessed | tf_op | source)
XLA Modules:
  0.0 565.6 jit_solution(13979629545272444692)
XLA Ops:
  0.7 2.8 reshape.411
  5.8 5.3 all-to-all-start
  11.1 3.1 collective-permute-start.1
  15.9 38.0 %small_gather.1 = f32[16,8,128]{2,1,0:T(8,128)} custom-call(f32[8,128]{1,0:T(8,128)} %bitcast_convert_fusion.x_ref), custom_call_target="tpu_custom_call" | custom-call | tf_op jit(solution)/shard_map/small_gather/pallas_call | solution.py:430
  58.4 16.0 %team_gather.4 = bf16[8,128,1152]{2,1,0:T(8,128)(2,1)} custom-call(bf16[128,1152]{1,0:T(8,128)(2,1)} %get-tuple-element.91.x_ref), custom_call_target="tpu_custom_call" | custom-call | tf_op jit(solution)/shard_map/team_gather/pallas_call | solution.py:252
  78.2 16.3 %team_gather.6 = bf16[8,128,1152]{2,1,0:T(8,128)(2,1)} custom-call(bf16[128,1152]{1,0:T(8,128)(2,1)} %get-tuple-element.90.x_ref), custom_call_target="tpu_custom_call" | custom-call | tf_op jit(solution)/shard_map/team_gather/pallas_call | solution.py:252
  95.4 4.4 all-to-all-start.1
  101.8 3.0 collective-permute-start
  104.8 2.3 broadcast_select_fusion.3
  107.1 11.0 %all-to-all-done.1 = bf16[8,72,576]{2,1,0:T(8,128)(2,1)} async-done(((bf16[8,72,576]{2,1,0:T(8,128)(2,1)}), bf16[8,72,576]{2,1,0:T(8,128)(2,1)}, u32[]{:S(2)}, u32[]{:S(2)}) %all-to-all-start.1) | async-done | bytes 663584 | tf_op jit(solution)/shard_map/all_to_all | solution.py:558
  118.1 29.7 %collective-permute-done = bf16[8,72,434]{2,1,0:T(8,128)(2,1)} collective-permute-done((bf16[8,72,434]{2,1,0:T(8,128)(2,1)}, bf16[8,72,434]{2,1,0:T(8,128)(2,1)}, u32[]{:S(2)}, u32[]{:S(2)}) %collective-permute-start) | collective-permute-done | bytes 500000 | tf_op jit(solution)/shard_map/ppermute | solution.py:527
  154.2 4.5 fusion.43
  162.5 3.5 fusion.4.q_ref.k_ref.v_ref
  166.0 6.5 %attend.1 = bf16[1024,256]{1,0:T(8,128)(2,1)} custom-call(bf16[1024,768]{1,0:T(8,128)(2,1)} %fusion.4.q_ref.k_ref.v_ref, bf16[1024,768]{1,0:T(8,128)(2,1)} %fusion.4.q_ref.k_ref.v_ref, bf16[1024,768]{1,0:T(8,128)(2,1)} %fusion.4.q_ref.k_ref.v_ref, f32[2,1024,1]{2,1,0:T(8,128)} %copy.161.gcol_ref, f32[2,1,1024]{2,1,0:T(1,128)} %broadcast_in_dim.96.grow_ref), custom_call_target="tpu_custom_call" | custom-call | flops 1073741824 | bytes 2097152 | tf_op jit(solution)/shard_map/attend/pallas_call | solution.py:119
  175.4 3.3 convolution_convert_fusion.3
  178.8 17.1 %team_scatter.4 = f32[128,1152]{1,0:T(8,128)} custom-call(bf16[8,128,1152]{2,1,0:T(8,128)(2,1)} %bitcast.209), custom_call_target="tpu_custom_call" | custom-call | tf_op jit(solution)/shard_map/team_scatter/pallas_call | solution.py:336
  198.3 16.1 %team_gather.5 = bf16[8,128,1152]{2,1,0:T(8,128)(2,1)} custom-call(bf16[128,1152]{1,0:T(8,128)(2,1)} %add_convert_fusion.3.x_ref), custom_call_target="tpu_custom_call" | custom-call | tf_op jit(solution)/shard_map/team_gather/pallas_call | solution.py:252
  214.4 1.6 broadcast_select_fusion.1
  216.5 1.7 fusion.103
  218.3 3.3 convolution_convert_fusion.6
  221.6 3.6 convert_reduce_fusion
  225.2 3.7 convolution_convert_fusion.1
  228.9 22.6 %team_scatter.6 = f32[128,1152]{1,0:T(8,128)} custom-call(bf16[8,128,1152]{2,1,0:T(8,128)(2,1)} %bitcast.234), custom_call_target="tpu_custom_call" | custom-call | tf_op jit(solution)/shard_map/team_scatter/pallas_call | solution.py:336
  251.5 2.0 multiply_reduce_fusion.9
  257.1 15.8 %team_gather.7 = bf16[8,128,1152]{2,1,0:T(8,128)(2,1)} custom-call(bf16[128,1152]{1,0:T(8,128)(2,1)} %get-tuple-element.48.x_ref), custom_call_target="tpu_custom_call" | custom-call | tf_op jit(solution)/shard_map/team_gather/pallas_call | solution.py:252
  272.9 3.9 multiply_reduce_fusion
  279.3 12.0 %attend_back.1 = (f32[1024,256]{1,0:T(8,128)}, f32[1024,256]{1,0:T(8,128)}, f32[1024,256]{1,0:T(8,128)}, f32[2,1024,1]{2,1,0:T(8,128)}, f32[2,1,1024]{2,1,0:T(1,128)}) custom-call(bf16[1024,768]{1,0:T(8,128)(2,1)} %fusion.4.q_ref.k_ref.v_ref, bf16[1024,768]{1,0:T(8,128)(2,1)} %fusion.4.q_ref.k_ref.v_ref, bf16[1024,768]{1,0:T(8,128)(2,1)} %fusion.4.q_ref.k_ref.v_ref, ...), custom_call_target="tpu_custom_call" | custom-call | flops 2684354560 | bytes 5242880 | tf_op jit(solution)/shard_map/attend_back/pallas_call | solution.py:136
  291.3 2.2 convert_element_type.194
  293.5 2.7 select_convert_fusion.1
  296.6 4.2 convert_reduce_fusion.4
  300.9 4.0 convolution_convert_fusion.4
  304.8 4.3 convolution_convert_fusion
  310.7 4.6 all-to-all-start.3
  315.9 19.7 %team_scatter.7 = f32[128,1152]{1,0:T(8,128)} custom-call(bf16[8,128,1152]{2,1,0:T(8,128)(2,1)} %bitcast.233), custom_call_target="tpu_custom_call" | custom-call | tf_op jit(solution)/shard_map/team_scatter/pallas_call | solution.py:336
  337.0 2.2 fusion.56
  339.8 4.1 concatenate.45
  345.1 3.6 all-to-all-start.5
  348.8 3.1 pad_maximum_fusion
  351.8 3.3 copy.167
  357.7 4.9 convolution_convert_fusion.5
  362.6 4.1 convolution_convert_fusion.2
  366.7 13.6 %all-to-all-done.5 = bf16[2,288,1152]{2,1,0:T(8,128)(2,1)S(1)} async-done(((bf16[2,288,1152]{2,1,0:T(8,128)(2,1)}), bf16[2,288,1152]{2,1,0:T(8,128)(2,1)S(1)}, u32[]{:S(2)}, u32[]{:S(2)}) %all-to-all-start.5) | async-done | bytes 1327136 | tf_op jit(solution)/shard_map/all_to_all | solution.py:687
  380.3 4.4 all-to-all-start.2
  386.0 2.6 copy.171
  388.8 28.4 %team_scatter.5 = f32[128,1152]{1,0:T(8,128)} custom-call(bf16[8,128,1152]{2,1,0:T(8,128)(2,1)} %bitcast.232), custom_call_target="tpu_custom_call" | custom-call | tf_op jit(solution)/shard_map/team_scatter/pallas_call | solution.py:336
  418.9 2.6 fusion.48
  421.6 5.0 all-to-all-start.4
  430.2 46.3 %small_sum.2 = f32[32,16,128]{2,1,0:T(8,128)} custom-call(f32[32,16,128]{2,1,0:T(8,128)} %bitcast.243), custom_call_target="tpu_custom_call" | custom-call | tf_op jit(solution)/shard_map/small_sum/pallas_call | solution.py:464
  482.9 17.2 %small_sum.3 = f32[32,8,128]{2,1,0:T(8,128)} custom-call(f32[32,8,128]{2,1,0:T(8,128)} %pad_bitcast_fusion.x_ref), custom_call_target="tpu_custom_call" | custom-call | tf_op jit(solution)/shard_map/small_sum/pallas_call | solution.py:464
  501.5 3.0 fusion.70
  511.4 2.1 collective-permute-done.5
  513.4 1.7 convert_add_fusion.3
  515.1 2.5 reduce_sum.386
  521.0 6.6 %collective-permute-done.7 = bf16[288,1152]{1,0:T(8,128)(2,1)} collective-permute-done((bf16[288,1152]{1,0:T(8,128)(2,1)S(1)}, bf16[288,1152]{1,0:T(8,128)(2,1)}, u32[]{:S(2)}, u32[]{:S(2)}) %collective-permute-start.7) | collective-permute-done | bytes 663584 | tf_op jit(solution)/shard_map/ppermute | solution.py:674
  527.7 2.3 convert_add_fusion.1
  530.0 10.3 %collective-permute-done.4 = bf16[8,72,434]{2,1,0:T(8,128)(2,1)} collective-permute-done((bf16[8,72,434]{2,1,0:T(8,128)(2,1)}, bf16[8,72,434]{2,1,0:T(8,128)(2,1)}, u32[]{:S(2)}, u32[]{:S(2)}) %collective-permute-start.4) | collective-permute-done | bytes 500000 | tf_op jit(solution)/shard_map/ppermute | solution.py:674
  541.6 2.7 reshape.456
  544.3 2.0 copy.168
  546.3 1.9 reshape.457
  550.0 5.2 collective-permute-done.6
  555.3 2.6 convert_add_fusion
  557.9 2.6 reshape.462
  560.5 1.8 copy.172
  562.2 3.0 reshape.463
  (296 shorter events, 72.8 us)
Async XLA Ops:
  0.6 14.2 %copy-start = (bf16[1152,432]{0,1:T(8,128)(2,1)S(1)}, bf16[1152,432]{0,1:T(8,128)(2,1)}, u32[]{:S(2)}) copy-start(bf16[1152,432]{0,1:T(8,128)(2,1)} %param.20) | copy-start | bytes 2985988
  4.1 10.7 %copy-start.29 = (bf16[2,1152]{1,0:T(2,128)(2,1)S(1)}, bf16[2,1152]{1,0:T(2,128)(2,1)}, u32[]{:S(2)}) copy-start(bf16[2,1152]{1,0:T(2,128)(2,1)} %param.18) | copy-start | bytes 13828
  4.2 10.7 %copy-start.54 = (f32[432]{0:T(512)S(1)}, f32[432]{0:T(512)}, u32[]{:S(2)}) copy-start(f32[432]{0:T(512)} %param.21) | copy-start | bytes 5188
  4.6 50.5 %copy-start.1 = (bf16[4,32,1152]{2,1,0:T(8,128)(2,1)S(1)}, bf16[4,32,1152]{2,1,0:T(8,128)(2,1)}, u32[]{:S(2)}) copy-start(bf16[4,32,1152]{2,1,0:T(8,128)(2,1)} %param.17) | copy-start | bytes 884740
  4.8 50.7 %copy-start.64 = (s32[2]{0:T(128)S(1)}, s32[2]{0:T(128)}, u32[]{:S(2)}) copy-start(s32[2]{0:T(128)} %param.19) | copy-start | bytes 28
  4.8 52.0 %copy-start.28 = (f32[9,1152]{1,0:T(8,128)S(1)}, f32[9,1152]{1,0:T(8,128)}, u32[]{:S(2)}) copy-start(f32[9,1152]{1,0:T(8,128)} %param.25) | copy-start | bytes 124420
  4.8 52.1 %copy-start.41 = (f32[1152]{0:T(1024)S(1)}, f32[1152]{0:T(1024)}, u32[]{:S(2)}) copy-start(f32[1152]{0:T(1024)} %param.26) | copy-start | bytes 13828
  4.9 52.5 %copy-start.7 = (bf16[4,32,1152]{2,1,0:T(8,128)(2,1)S(1)}, bf16[4,32,1152]{2,1,0:T(8,128)(2,1)}, u32[]{:S(2)}) copy-start(bf16[4,32,1152]{2,1,0:T(8,128)(2,1)} %param.33) | copy-start | bytes 884740
  5.8 89.6 %all-to-all-start = ((bf16[8,72,434]{2,1,0:T(8,128)(2,1)}), bf16[8,72,434]{2,1,0:T(8,128)(2,1)}, u32[]{:S(2)}, u32[]{:S(2)}) async-start(bf16[8,72,434]{2,1,0:T(8,128)(2,1)} %pad_maximum_fusion.8), calls=%async_computation | async-start | bytes 1179648 | tf_op jit(solution)/shard_map/all_to_all | solution.py:542
  11.1 88.8 %collective-permute-start.1 = (bf16[72,1152]{1,0:T(8,128)(2,1)}, bf16[72,1152]{1,0:T(8,128)(2,1)}, u32[]{:S(2)}, u32[]{:S(2)}) collective-permute-start(bf16[72,1152]{1,0:T(8,128)(2,1)} %param.27), channel_id=1, source_target_pairs={{0,8},{8,0},{1,9},{9,1},{2,10},{10,2},{3,11},{11,3},{4,12},{12,4},... | collective-permute-start | bytes 497672 | tf_op jit(solution)/shard_map/ppermute | solution.py:527
  14.1 90.6 %collective-permute-start.3 = (bf16[288,1152]{1,0:T(8,128)(2,1)}, bf16[288,1152]{1,0:T(8,128)(2,1)}, u32[]{:S(2)}, u32[]{:S(2)}) collective-permute-start(bf16[288,1152]{1,0:T(8,128)(2,1)} %param.31), channel_id=1, source_target_pairs={{0,8},{8,0},{1,9},{9,1},{2,10},{10,2},{3,11},{11,3},{4,12},{12,4},... | collective-permute-start | bytes 1990664 | tf_op jit(solution)/shard_map/ppermute | solution.py:527
  14.2 144.5 %copy-start.50 = (s32[1024]{0:T(1024)}, s32[1024]{0:T(1024)S(1)}, u32[]{:S(2)}) copy-start(s32[1024]{0:T(1024)S(1)} %fusion.75) | copy-start | bytes 12292
  55.1 19.3 %copy-start.65 = (f32[16]{0:T(128)S(1)}, f32[16]{0:T(128)}, u32[]{:S(2)}) copy-start(f32[16]{0:T(128)} %param.24) | copy-start | bytes 196
  55.2 19.6 %copy-start.18 = (bf16[72,4608]{1,0:T(8,128)(2,1)S(1)}, bf16[72,4608]{1,0:T(8,128)(2,1)}, u32[]{:S(2)}) copy-start(bf16[72,4608]{1,0:T(8,128)(2,1)} %param.29) | copy-start | bytes 1990660
  56.8 105.7 %copy-start.44 = (pred[1024]{0:T(1024)(128)(4,1)}, pred[1024]{0:T(1024)(128)(4,1)S(1)}, u32[]{:S(2)}) copy-start(pred[1024]{0:T(1024)(128)(4,1)S(1)} %iota_compare_fusion.3) | copy-start | bytes 3076
  57.2 279.7 %copy-start.37 = (f32[128]{0:T(128)}, f32[128]{0:T(128)S(1)}, u32[]{:S(2)}) copy-start(f32[128]{0:T(128)S(1)} %div.59) | copy-start | bytes 1540
  57.3 279.7 %copy-start.42 = (f32[128]{0:T(128)}, f32[128]{0:T(128)S(1)}, u32[]{:S(2)}) copy-start(f32[128]{0:T(128)S(1)} %rsqrt.22) | copy-start | bytes 1540
  76.7 17.9 %copy-start.36 = (f32[4608]{0:T(1024)S(1)}, f32[4608]{0:T(1024)}, u32[]{:S(2)}) copy-start(f32[4608]{0:T(1024)} %param.30) | copy-start | bytes 55300
  94.5 10.2 %copy-start.19 = (bf16[288,1152]{1,0:T(8,128)(2,1)S(1)}, bf16[288,1152]{1,0:T(8,128)(2,1)}, u32[]{:S(2)}) copy-start(bf16[288,1152]{1,0:T(8,128)(2,1)} %param.31) | copy-start | bytes 1990660
  94.7 126.9 %copy-start.47 = (f32[576]{0:T(1024)}, f32[576]{0:T(1024)S(1)}, u32[]{:S(2)}) copy-start(f32[576]{0:T(1024)S(1)} %add.307) | copy-start | bytes 6916
  95.4 22.6 %all-to-all-start.1 = ((bf16[8,72,576]{2,1,0:T(8,128)(2,1)}), bf16[8,72,576]{2,1,0:T(8,128)(2,1)}, u32[]{:S(2)}, u32[]{:S(2)}) async-start(bf16[8,72,576]{2,1,0:T(8,128)(2,1)} %reshape.425), calls=%async_computation.1 | async-start | bytes 1474560 | tf_op jit(solution)/shard_map/all_to_all | solution.py:558
  101.8 45.9 %collective-permute-start = (bf16[8,72,434]{2,1,0:T(8,128)(2,1)}, bf16[8,72,434]{2,1,0:T(8,128)(2,1)}, u32[]{:S(2)}, u32[]{:S(2)}) collective-permute-start(bf16[8,72,434]{2,1,0:T(8,128)(2,1)} %all-to-all-done), channel_id=1, source_target_pairs={{0,8},{8,0},{1,9},{9,1},{2,10},{10,2},{3,11},{11,3},{4,12},{12,4},... | collective-permute-start | bytes 1499912 | tf_op jit(solution)/shard_map/ppermute | solution.py:527
  118.1 96.4 %collective-permute-start.2 = (bf16[8,72,576]{2,1,0:T(8,128)(2,1)}, bf16[8,72,576]{2,1,0:T(8,128)(2,1)}, u32[]{:S(2)}, u32[]{:S(2)}) collective-permute-start(bf16[8,72,576]{2,1,0:T(8,128)(2,1)} %all-to-all-done.1), channel_id=1, source_target_pairs={{0,8},{8,0},{1,9},{9,1},{2,10},{10,2},{3,11},{11,3},{4,12},{12,4},... | collective-permute-start | bytes 1990664 | tf_op jit(solution)/shard_map/ppermute | solution.py:527
  152.9 5.9 %copy-start.14 = (bf16[1152,6,128]{0,2,1:T(8,128)(2,1)}, bf16[1152,6,128]{0,2,1:T(8,128)(2,1)S(1)}, u32[]{:S(2)}) copy-start(bf16[1152,6,128]{0,2,1:T(8,128)(2,1)S(1)} %pad.47) | copy-start | bytes 5308420
  175.4 20.5 %copy-start.30 = (f32[1152]{0:T(1024)S(1)}, f32[1152]{0:T(1024)}, u32[]{:S(2)}) copy-start(f32[1152]{0:T(1024)} %param.28) | copy-start | bytes 13828
  254.8 22.0 %copy-start.55 = (f32[128]{0:T(128)}, f32[128]{0:T(128)S(1)}, u32[]{:S(2)}) copy-start(f32[128]{0:T(128)S(1)} %negate_multiply_fusion.1) | copy-start | bytes 1540
  279.3 14.2 %copy-start.45 = (pred[1024]{0:T(1024)(128)(4,1)S(1)}, pred[1024]{0:T(1024)(128)(4,1)}, u32[]{:S(2)}) copy-start(pred[1024]{0:T(1024)(128)(4,1)} %copy-done.44) | copy-start | bytes 3076
  291.3 4.9 copy-start.16
  296.6 4.3 copy-start.9
  310.7 34.4 %all-to-all-start.3 = ((bf16[2,72,1152]{2,1,0:T(8,128)(2,1)}), bf16[2,72,1152]{2,1,0:T(8,128)(2,1)}, u32[]{:S(2)}, u32[]{:S(2)}) async-start(bf16[2,72,1152]{2,1,0:T(8,128)(2,1)} %slice.396), calls=%async_computation.3 | async-start | bytes 663552 | tf_op jit(solution)/shard_map/all_to_all | solution.py:697
  345.1 35.2 %all-to-all-start.5 = ((bf16[2,288,1152]{2,1,0:T(8,128)(2,1)}), bf16[2,288,1152]{2,1,0:T(8,128)(2,1)S(1)}, u32[]{:S(2)}, u32[]{:S(2)}) async-start(bf16[2,288,1152]{2,1,0:T(8,128)(2,1)} %bitcast.242), calls=%async_computation.5 | async-start | bytes 2654208 | tf_op jit(solution)/shard_map/all_to_all | solution.py:687
  357.7 4.9 copy-start.21
  357.7 4.9 copy-start.23
  357.7 4.9 copy-start.48
  357.7 4.9 copy-start.68
  380.3 5.7 %copy-start.4 = (bf16[2,288,1152]{2,1,0:T(8,128)(2,1)}, bf16[2,288,1152]{2,1,0:T(8,128)(2,1)S(1)}, u32[]{:S(2)}) copy-start(bf16[2,288,1152]{2,1,0:T(8,128)(2,1)S(1)} %all-to-all-done.5) | copy-start | bytes 3981316
  380.3 41.3 %all-to-all-start.2 = ((bf16[16,72,434]{2,1,0:T(8,128)(2,1)}), bf16[16,72,434]{2,1,0:T(8,128)(2,1)}, u32[]{:S(2)}, u32[]{:S(2)}) async-start(bf16[16,72,434]{2,1,0:T(8,128)(2,1)} %copy.167), calls=%async_computation.2 | async-start | bytes 2359296 | tf_op jit(solution)/shard_map/all_to_all | solution.py:679
  388.6 30.1 %copy-start.39 = (f32[9,2,128]{2,1,0:T(2,128)S(1)}, f32[9,2,128]{2,1,0:T(2,128)}, u32[]{:S(2)}) copy-start(f32[9,2,128]{2,1,0:T(2,128)} %constant_dynamic-update-slice_fusion.7) | copy-start | bytes 27652
  388.6 30.1 %copy-start.62 = (f32[256]{0:T(256)S(1)}, f32[256]{0:T(256)}, u32[]{:S(2)}) copy-start(f32[256]{0:T(256)} %get-tuple-element.29) | copy-start | bytes 3076
  388.6 30.1 %copy-start.61 = (f32[256]{0:T(256)S(1)}, f32[256]{0:T(256)}, u32[]{:S(2)}) copy-start(f32[256]{0:T(256)} %get-tuple-element.30) | copy-start | bytes 3076
  388.6 30.2 %copy-start.60 = (f32[256]{0:T(256)S(1)}, f32[256]{0:T(256)}, u32[]{:S(2)}) copy-start(f32[256]{0:T(256)} %get-tuple-element.31) | copy-start | bytes 3076
  388.7 30.2 %copy-start.59 = (f32[256]{0:T(256)S(1)}, f32[256]{0:T(256)}, u32[]{:S(2)}) copy-start(f32[256]{0:T(256)} %get-tuple-element.32) | copy-start | bytes 3076
  388.7 30.2 %copy-start.58 = (f32[256]{0:T(256)S(1)}, f32[256]{0:T(256)}, u32[]{:S(2)}) copy-start(f32[256]{0:T(256)} %get-tuple-element.26) | copy-start | bytes 3076
  388.7 30.2 %copy-start.2 = (f32[128,1152]{1,0:T(8,128)S(1)}, f32[128,1152]{1,0:T(8,128)}, u32[]{:S(2)}) copy-start(f32[128,1152]{1,0:T(8,128)} %team_scatter.7) | copy-start | bytes 1769476
  388.7 30.2 %copy-start.5 = (f32[128,1152]{1,0:T(8,128)S(1)}, f32[128,1152]{1,0:T(8,128)}, u32[]{:S(2)}) copy-start(f32[128,1152]{1,0:T(8,128)} %team_scatter.4) | copy-start | bytes 1769476
  388.7 30.2 %copy-start.38 = (f32[128]{0:T(128)S(1)}, f32[128]{0:T(128)}, u32[]{:S(2)}) copy-start(f32[128]{0:T(128)} %copy-done.37) | copy-start | bytes 1540
  388.7 30.2 %copy-start.40 = (f32[1152]{0:T(1024)S(1)}, f32[1152]{0:T(1024)}, u32[]{:S(2)}) copy-start(f32[1152]{0:T(1024)} %param.32) | copy-start | bytes 13828
  388.7 30.2 %copy-start.43 = (f32[128]{0:T(128)S(1)}, f32[128]{0:T(128)}, u32[]{:S(2)}) copy-start(f32[128]{0:T(128)} %copy-done.42) | copy-start | bytes 1540
  388.7 30.2 %copy-start.53 = (f32[128]{0:T(128)S(1)}, f32[128]{0:T(128)}, u32[]{:S(2)}) copy-start(f32[128]{0:T(128)} %copy-done.52) | copy-start | bytes 1540
  388.7 30.2 %copy-start.56 = (f32[128]{0:T(128)S(1)}, f32[128]{0:T(128)}, u32[]{:S(2)}) copy-start(f32[128]{0:T(128)} %copy-done.55) | copy-start | bytes 1540
  388.8 30.2 %copy-start.63 = (f32[128]{0:T(128)S(1)}, f32[128]{0:T(128)}, u32[]{:S(2)}) copy-start(f32[128]{0:T(128)} %negate_multiply_fusion) | copy-start | bytes 1540
  421.6 5.1 copy-start.35
  421.6 5.5 copy-start.32
  421.6 5.5 copy-start.31
  421.6 6.0 %copy-start.66 = (f32[2]{0:T(128)S(1)}, f32[2]{0:T(128)}, u32[]{:S(2)}) copy-start(f32[2]{0:T(128)} %get-tuple-element.85) | copy-start | bytes 28
  421.6 6.3 %copy-start.49 = (f32[576]{0:T(1024)S(1)}, f32[576]{0:T(1024)}, u32[]{:S(2)}) copy-start(f32[576]{0:T(1024)} %get-tuple-element.88) | copy-start | bytes 6916
  421.6 6.4 %copy-start.33 = (f32[1152]{0:T(1024)S(1)}, f32[1152]{0:T(1024)}, u32[]{:S(2)}) copy-start(f32[1152]{0:T(1024)} %get-tuple-element.47) | copy-start | bytes 13828
  421.6 6.4 %copy-start.34 = (f32[1152]{0:T(1024)S(1)}, f32[1152]{0:T(1024)}, u32[]{:S(2)}) copy-start(f32[1152]{0:T(1024)} %convert_reduce_fusion.2) | copy-start | bytes 13828
  421.6 96.5 %all-to-all-start.4 = ((bf16[16,72,576]{2,1,0:T(8,128)(2,1)}), bf16[16,72,576]{2,1,0:T(8,128)(2,1)S(1)}, u32[]{:S(2)}, u32[]{:S(2)}) async-start(bf16[16,72,576]{2,1,0:T(8,128)(2,1)} %bitcast.215), calls=%async_computation.4 | async-start | bytes 2949120 | tf_op jit(solution)/shard_map/all_to_all | solution.py:679
  506.2 7.3 %collective-permute-start.5 = (bf16[72,1152]{1,0:T(8,128)(2,1)S(1)}, bf16[72,1152]{1,0:T(8,128)(2,1)}, u32[]{:S(2)}, u32[]{:S(2)}) collective-permute-start(bf16[72,1152]{1,0:T(8,128)(2,1)S(1)} %reduce_sum.387), channel_id=1, source_target_pairs={{0,16},{16,0},{1,17},{17,1},{2,18},{18,2},{3,19},{19,3},{4,20},{20... | collective-permute-start | bytes 497672 | tf_op jit(solution)/shard_map/ppermute | solution.py:674
  508.4 19.2 %collective-permute-start.7 = (bf16[288,1152]{1,0:T(8,128)(2,1)S(1)}, bf16[288,1152]{1,0:T(8,128)(2,1)}, u32[]{:S(2)}, u32[]{:S(2)}) collective-permute-start(bf16[288,1152]{1,0:T(8,128)(2,1)S(1)} %reduce_sum.389), channel_id=1, source_target_pairs={{0,16},{16,0},{1,17},{17,1},{2,18},{18,2},{3,19},{19,3},{4,20},{20... | collective-permute-start | bytes 1990664 | tf_op jit(solution)/shard_map/ppermute | solution.py:674
  517.6 22.7 %collective-permute-start.4 = (bf16[8,72,434]{2,1,0:T(8,128)(2,1)}, bf16[8,72,434]{2,1,0:T(8,128)(2,1)}, u32[]{:S(2)}, u32[]{:S(2)}) collective-permute-start(bf16[8,72,434]{2,1,0:T(8,128)(2,1)} %reduce_sum.386), channel_id=1, source_target_pairs={{0,16},{16,0},{1,17},{17,1},{2,18},{18,2},{3,19},{19,3},{4,20},{20... | collective-permute-start | bytes 1499912 | tf_op jit(solution)/shard_map/ppermute | solution.py:674
  519.5 20.8 %copy-start.13 = (bf16[8,72,434]{2,1,0:T(8,128)(2,1)S(1)}, bf16[8,72,434]{2,1,0:T(8,128)(2,1)}, u32[]{:S(2)}) copy-start(bf16[8,72,434]{2,1,0:T(8,128)(2,1)} %reduce_sum.386) | copy-start | bytes 1499908
  519.5 35.8 %collective-permute-start.6 = (bf16[8,72,576]{2,1,0:T(8,128)(2,1)}, bf16[8,72,576]{2,1,0:T(8,128)(2,1)}, u32[]{:S(2)}, u32[]{:S(2)}) collective-permute-start(bf16[8,72,576]{2,1,0:T(8,128)(2,1)} %reduce_sum.388), channel_id=1, source_target_pairs={{0,16},{16,0},{1,17},{17,1},{2,18},{18,2},{3,19},{19,3},{4,20},{20... | collective-permute-start | bytes 1990664 | tf_op jit(solution)/shard_map/ppermute | solution.py:674
  (23 other events, 72.8 us)

commit v3 on v2

--- a/solution.py
+++ b/solution.py
@@ -437,6 +437,46 @@
         name="small_gather",
     )(padded)
     return out.reshape(total, lines * 128)[:, :count]
+
+
+def small_scatter_kernel(sizes, x_ref, out_ref, came, send_sem, recv_sem):
+    halves, groups = sizes
+    total = halves * groups * TEAM
+    line = groups * TEAM
+    me = flat_index(sizes)
+    greet_all(me, total, sizes)
+    came[me] = x_ref[me % line]
+    send_all(
+        me, total, sizes, lambda peer: x_ref.at[peer % line], came.at[me], send_sem, recv_sem, came
+    )
+
+    def item(number, carry):
+        out_ref[number] = jnp.sum(came[pl.ds(number * TEAM, TEAM)], axis=0)
+        return carry
+
+    lax.fori_loop(0, halves * groups, item, 0)
+
+
+def small_scatter(source, sizes, number):
+    halves, groups = sizes
+    line, count = source.shape
+    lines = -(-count // 1024) * 8
+    padded = jnp.pad(source, ((0, 0), (0, lines * 128 - count))).reshape(line, lines, 128)
+    vmem = pl.BlockSpec(memory_space=pltpu.VMEM)
+    out = pl.pallas_call(
+        functools.partial(small_scatter_kernel, sizes),
+        out_shape=jax.ShapeDtypeStruct((halves * groups, lines, 128), F32),
+        in_specs=[vmem],
+        out_specs=vmem,
+        scratch_shapes=[
+            pltpu.VMEM((halves * line, lines, 128), F32),
+            pltpu.SemaphoreType.DMA,
+            pltpu.SemaphoreType.DMA,
+        ],
+        compiler_params=pltpu.CompilerParams(collective_id=number, has_side_effects=True),
+        name="small_scatter",
+    )(padded)
+    return out.reshape(halves * groups, lines * 128)[:, :count]
 
 
 def small_sum_kernel(sizes, x_ref, out_ref, came, summed, sems):
@@ -512,15 +552,15 @@
 
     condition_float = condition.astype(F32)
     squashed = jax.nn.silu(condition_float).astype(BF16)
+    squashed_other = lax.ppermute(squashed, "items", [(0, 1), (1, 0)])
+    squashed_every = jnp.concatenate(
+        [
+            jnp.where(half == 0, squashed, squashed_other),
+            jnp.where(half == 0, squashed_other, squashed),
+        ],
+        axis=0,
+    )
     modulation_piece = (dot(squashed, modulator) + baseline).astype(BF16).T
-    modulation_all = small_gather(
-        modulation_piece.T.astype(F32).reshape(-1), (1, groups), 3
-    ).reshape(devices, groups, columns)
-    modulation = pick(modulation_all, 1, group).reshape(-1)
-    shift_one, scale_one, gate_one, shift_two, scale_two, gate_two = [
-        modulation[part * D : (part + 1) * D] for part in range(6)
-    ]
-
     def group_gather(source):
         if groups != 2:
             return lax.all_gather(source, "grp", axis=0, tiled=True)
@@ -540,7 +580,18 @@
         axis=2,
     )
     project_part = lax.all_to_all(project_cut, "pos", split_axis=0, concat_axis=0, tiled=True)
+    project_part, modulation_piece, expander, reducer, combiner = lax.optimization_barrier(
+        (project_part, modulation_piece, expander, reducer, combiner)
+    )
     project_mine = group_gather(project_part).reshape(D, -1)
+    modulation_all = small_gather(
+        modulation_piece.T.astype(F32).reshape(-1), (1, groups), 3
+    ).reshape(devices, groups, columns)
+    modulation = pick(modulation_all, 1, group).reshape(-1)
+    shift_one, scale_one, gate_one, shift_two, scale_two, gate_two = [
+        modulation[part * D : (part + 1) * D] for part in range(6)
+    ]
+
     project_wide = jnp.concatenate(
         [
             pad_heads(project_mine[:, : 3 * HEADS * HD].reshape(D, 3 * HEADS, HD), 2).reshape(
@@ -605,16 +656,42 @@
     reduced = team_scatter(dot(activated, reduce_mine)) + leveling
     block_output = (middle + gate_two * reduced).astype(BF16).reshape(ROWS_DEV, GRID, D)
 
+    def swap_add(share):
+        low = share.astype(BF16)
+        other = lax.ppermute(low, "items", [(0, 1), (1, 0)])
+        return low.astype(F32) + other.astype(F32)
+
+    def to_owners(source):
+        pieces = source.reshape(devices, depth, source.shape[1])
+        arrived = lax.all_to_all(pieces, rows_axes, split_axis=0, concat_axis=0, tiled=True)
+        arrived = arrived.reshape(groups, TEAM, depth, source.shape[1])
+        return jnp.sum(arrived.astype(F32), axis=0).astype(BF16)
+
+    def group_scatter(source):
+        low = source.astype(BF16)
+        if groups != 2:
+            arrived = lax.all_to_all(low, "grp", split_axis=0, concat_axis=0, tiled=True)
+            return jnp.sum(arrived.astype(F32), axis=0)
+        arrived = lax.ppermute(pick(low, 0, 1 - group), "grp", [(0, 1), (1, 0)])
+        return pick(low, 0, group).astype(F32) + arrived.astype(F32)
+
     gate_two_grad = jnp.sum(upstream * reduced, axis=0)
     reduced_grad = (gate_two * upstream).astype(BF16)
     leveling_grad = jnp.sum(reduced_grad.astype(F32), axis=0)
     reduced_grad_all = team_gather(reduced_grad)
     reducer_grad = outer_sum(activated, reduced_grad_all)
+    reducer_out = swap_add(group_scatter(reducer_grad.reshape(groups, inner, D)))
     activated_grad = back_dot(reduced_grad_all, reduce_mine)
     pull = jax.vjp(lambda v: jax.nn.gelu(v, approximate=True), expanded)[1]
     expanded_grad = pull(activated_grad)[0].astype(BF16)
     thresholds_grad = jnp.sum(expanded_grad.astype(F32), axis=0)
     expander_grad = outer_sum(hidden_two_all, expanded_grad)
+    expander_out = swap_add(
+        to_owners(expander_grad.astype(BF16))
+        .reshape(TEAM, depth, groups, inner)
+        .transpose(1, 2, 0, 3)
+        .reshape(depth, FF)
+    )
     hidden_two_grad = team_scatter(back_dot(expanded_grad, expand_mine))
     second_pull = jax.vjp(modulate, middle, shift_two, scale_two)[1]
     middle_part, shift_two_grad, scale_two_grad = second_pull(hidden_two_grad)
@@ -624,6 +701,17 @@
     displacement_grad = jnp.sum(branch_grad.astype(F32), axis=0)
     branch_grad_all = team_gather(branch_grad)
     combiner_grad = outer_sum(smoothed, branch_grad_all)
+    combiner_low = combiner_grad.reshape(HEADS, LANES, D)[:, :HD]
+    if whole_heads:
+        combiner_share = group_scatter(combiner_low)
+    else:
+        placed = jnp.where(
+            (jnp.arange(TEAM) == place)[None, :, None, None], combiner_low[:, None], 0.0
+        )
+        combiner_share = lax.psum_scatter(
+            placed.reshape(D, D), rows_axes, scatter_dimension=0, tiled=True
+        )
+    combiner_out = swap_add(combiner_share)
     smoothed_grad = back_dot(branch_grad_all, combine_wide).astype(BF16).astype(F32)
     pedestal_grad = jnp.sum(smoothed_grad, axis=0)
     grad_grid = smoothed_grad.reshape(GRID, GRID, WIDE)
@@ -669,44 +757,6 @@
     inputs_part, shift_one_grad, scale_one_grad = first_pull(hidden_grad)
     patches_grad = (middle_grad + inputs_part).astype(BF16).reshape(ROWS_DEV, GRID, D)
 
-    def swap_add(share):
-        low = share.astype(BF16)
-        other = lax.ppermute(low, "items", [(i, (i + 1) % 2) for i in range(2)])
-        return low.astype(F32) + other.astype(F32)
-
-    def to_owners(source):
-        pieces = source.reshape(devices, depth, source.shape[1])
-        arrived = lax.all_to_all(pieces, rows_axes, split_axis=0, concat_axis=0, tiled=True)
-        arrived = arrived.reshape(groups, TEAM, depth, source.shape[1])
-        return swap_add(jnp.sum(arrived.astype(F32), axis=0))
-
-    expander_share = to_owners(expander_grad.astype(BF16))
-    expander_out = (
-        expander_share.reshape(TEAM, depth, groups, inner).transpose(1, 2, 0, 3).reshape(depth, FF)
-    )
-    reducer_pieces = lax.all_to_all(
-        reducer_grad.astype(BF16).reshape(groups, inner, D),
-        "grp",
-        split_axis=0,
-        concat_axis=0,
-        tiled=True,
-    )
-    reducer_out = swap_add(jnp.sum(reducer_pieces.astype(F32), axis=0))
-    combiner_low = combiner_grad.reshape(HEADS, LANES, D)[:, :HD].astype(BF16)
-    if whole_heads:
-        combiner_pieces = lax.all_to_all(
-            combiner_low, "grp", split_axis=0, concat_axis=0, tiled=True
-        )
-        combiner_share = jnp.sum(combiner_pieces.astype(F32), axis=0)
-    else:
-        placed = jnp.zeros((HEADS, TEAM, HD, D), F32)
-        placed = lax.dynamic_update_slice_in_dim(
-            placed, combiner_low.astype(F32)[:, None], place, 1
-        )
-        combiner_share = lax.psum_scatter(
-            placed.reshape(D, D), rows_axes, scatter_dimension=0, tiled=True
-        )
-    combiner_out = swap_add(combiner_share)
     projector_low = projector_grad.astype(BF16)
     project_share = to_owners(
         jnp.concatenate(
@@ -719,27 +769,15 @@
             axis=1,
         )
     )
-    projector_out = (
+    projector_out = swap_add(
         project_share[:, :, : 3 * HEADS * HD]
         .reshape(TEAM, depth, 3, HEADS, HD)
         .transpose(1, 2, 3, 0, 4)
         .reshape(depth, 3 * D)
     )
-    forgetter_out = project_share[:, :, 3 * HEADS * HD :].transpose(1, 2, 0).reshape(depth, H)
-
-    def spot(value, shape, axis, at):
-        return lax.dynamic_update_slice_in_dim(
-            jnp.zeros(shape, F32), jnp.expand_dims(value, axis), at, axis
-        ).reshape(-1)
-
-    def sum_everywhere(parts, number):
-        total = small_sum(jnp.concatenate(parts), (halves, groups), number)
-        split = []
-        start = 0
-        for part in parts:
-            split.append(total[start : start + part.shape[0]])
-            start += part.shape[0]
-        return split
+    forgetter_out = swap_add(
+        project_share[:, :, 3 * HEADS * HD :].transpose(1, 2, 0).reshape(depth, H)
+    )
 
     modulation_grad = jnp.concatenate(
         [
@@ -750,37 +788,37 @@
             scale_two_grad,
             gate_two_grad,
         ]
-    )
-    item = half * groups + group
-    here = ((group == 0) & (place == 0)).astype(F32)
-    split = sum_everywhere(
-        [
-            spot(modulation_grad, (halves * groups, 6 * D), 0, item),
-            spot(retention_grad, (HEADS, TEAM), 1, place),
-            spot(
-                tap_stack.reshape(9, HEADS, LANES)[:, :, :HD], (9, HEADS, TEAM, HD), 2, place
-            ),
-            spot(pedestal_grad.reshape(HEADS, LANES)[:, :HD], (HEADS, TEAM, HD), 1, place),
-            displacement_grad,
-            spot(thresholds_grad.reshape(groups, inner), (groups, TEAM, inner), 1, place),
-            leveling_grad,
-            spot(squashed.astype(F32) * here, (halves, groups, D), 0, half),
-        ],
-        4,
-    )
-    device = group * TEAM + place
-    rows_every = pick(split[0].reshape(halves * groups, devices, columns), 1, device)
-    squashed_every = split[7].reshape(halves * groups, D)
+    ).reshape(devices, columns)
+    rows_every = small_scatter(modulation_grad, (halves, groups), 4)
     modulator_out = lax.dot_general(
-        squashed_every, rows_every, (((0,), (0,)), ((), ())), precision=HIGH
+        squashed_every.astype(F32), rows_every, (((0,), (0,)), ((), ())), precision=HIGH
     )
     baseline_out = jnp.sum(rows_every, axis=0)
     modulation_rows = pick(rows_every.reshape(halves, groups, columns), 0, half)
     squashed_grad = jnp.dot(modulation_rows, modulator.astype(F32).T, precision=HIGH)
-    squashed_total = sum_everywhere(
-        [spot(squashed_grad, (halves, groups, D), 0, half)], 5
-    )[0]
-    squashed_sum = pick(squashed_total.reshape(halves, groups, D), 0, half)
+
+    def spot(value, shape, axis, at):
+        where = (jnp.arange(shape[axis]) == at).reshape(
+            [-1 if spot_axis == axis else 1 for spot_axis in range(len(shape))]
+        )
+        return jnp.where(where, jnp.expand_dims(value, axis), 0.0).reshape(-1)
+
+    parts = [
+        spot(squashed_grad, (halves, groups, D), 0, half),
+        spot(retention_grad, (HEADS, TEAM), 1, place),
+        spot(tap_stack.reshape(9, HEADS, LANES)[:, :, :HD], (9, HEADS, TEAM, HD), 2, place),
+        spot(pedestal_grad.reshape(HEADS, LANES)[:, :HD], (HEADS, TEAM, HD), 1, place),
+        displacement_grad,
+        spot(thresholds_grad.reshape(groups, inner), (groups, TEAM, inner), 1, place),
+        leveling_grad,
+    ]
+    total = small_sum(jnp.concatenate(parts), (halves, groups), 5)
+    split = []
+    start = 0
+    for part in parts:
+        split.append(total[start : start + part.shape[0]])
+        start += part.shape[0]
+    squashed_sum = pick(split[0].reshape(halves, groups, D), 0, half)
     silu_pull = jax.vjp(jax.nn.silu, condition_float)[1]
     condition_grad = silu_pull(squashed_sum)[0]
     return (

time: 574 us -> 520 us (0.906)
  waiting for transfers between devices: 78.5 us -> 23.3 us
  local copies, waits for them, and re-layouts: 65.8 us -> 71.6 us
    pallas_call x2 -> x1, Pallas kernels: 63.4 us -> 15.5 us  [small_sum(): pl.pallas_call(functools.partial(small_sum_kernel, sizes), out_shape=jax....]
    pallas_call x4, Pallas kernels: 64.3 us -> 110 us  [team_gather(): pl.pallas_call(team_gather_kernel, out_shape=jax.ShapeDtypeStruct((TEAM,...]
    ppermute x4, waiting for transfers between devices: 29.7 us -> 0.01 us  [group_gather(): other = lax.ppermute(source, 'grp', [(0, 1), (1, 0)])]
    pallas_call x1, Pallas kernels: 38 us -> 8.72 us  [small_gather(): pl.pallas_call(functools.partial(small_gather_kernel, sizes), out_shape=j...]
    pallas_call x4, Pallas kernels: 87.8 us -> 109 us  [team_scatter(): pl.pallas_call(team_scatter_kernel, out_shape=jax.ShapeDtypeStruct((rows,...]
    all_to_all x2 -> x0, waiting for transfers between devices: 13.6 us -> none  [the longest x1 13.6 us: on_device(): lax.all_to_all(reducer_grad.astype(BF16).reshape(groups, inner, D), 'grp'...]
    unnamed x158 -> x171, local copies, waits for them, and re-layouts: 11.7 us -> 24.5 us
    all_to_all x1, waiting for transfers between devices: 11 us -> 0.01 us  [on_device(): lax.all_to_all(expand_cut, 'pos', split_axis=0, concat_axis=0, tiled=True)]
  transfers between devices with their start and end apart: 14 -> 16, of which waited for: 7 -> 4; matrix products, arithmetic and copies ran while one was open for 20% -> 23% of each run, Pallas kernels for 39% -> 40%
where the time goes in v3:
time: 520 us; the launch traced here: 510 us
  Pallas kernels  271 us (52%)
  local copies, waits for them, and re-layouts  71.6 us (14%)
  other arithmetic  61.5 us (12%)
  matrix products  47.9 us (9%)
  starting transfers between devices  32.3 us (6%)
  waiting for transfers between devices  23.3 us (4%)
    pallas_call x4, Pallas kernels, team_gather(): pl.pallas_call(team_gather_kernel, out_shape=jax.ShapeDtypeStruct((TEAM,...  110 us
    pallas_call x4, Pallas kernels, team_scatter(): pl.pallas_call(team_scatter_kernel, out_shape=jax.ShapeDtypeStruct((rows,...  109 us
    unnamed x171, local copies, waits for them, and re-layouts  24.5 us
    ppermute x5, waiting for transfers between devices, swap_add(): other = lax.ppermute(low, 'items', [(0, 1), (1, 0)])  20 us
    dot_general x6, matrix products, dot(): return jnp.dot(left, right, preferred_element_type=F32)  15.7 us
    pallas_call x1, Pallas kernels, small_sum(): pl.pallas_call(functools.partial(small_sum_kernel, sizes), out_shape=jax....  15.5 us
    dot_general x4, matrix products, back_dot(): lax.dot_general(gradient, matrix, (((1,), (1,)), ((), ())), preferred_ele...  15.4 us
    pallas_call x1, Pallas kernels, attend_back(): pl.pallas_call(attend_back_kernel, grid=(HEADS,), out_shape=[jax.ShapeDty...  12 us
  transfers between devices with their start and end apart: 16, of which 4 were waited for; matrix products, arithmetic and copies ran while one was open for 23% of the time, Pallas kernels for 40%

profile of v3, /device:TPU:0, one launch (start us, length us, event | category | flops | bytes accessed | tf_op | source)
XLA Modules:
  0.0 509.8 jit_solution(3398143945921998485)
XLA Ops:
  0.7 2.8 reshape.431
  5.8 5.3 %all-to-all-start = ((bf16[8,72,434]{2,1,0:T(8,128)(2,1)}), bf16[8,72,434]{2,1,0:T(8,128)(2,1)}, u32[]{:S(2)}, u32[]{:S(2)}) async-start(bf16[8,72,434]{2,1,0:T(8,128)(2,1)} %pad_maximum_fusion.8), calls=%async_computation | async-start | bytes 1179648 | tf_op jit(solution)/shard_map/all_to_all | solution.py:582
  11.2 1.9 collective-permute-start.4
  22.9 8.7 %small_gather.1 = f32[16,8,128]{2,1,0:T(8,128)} custom-call(f32[8,128]{1,0:T(8,128)} %bitcast_convert_fusion.x_ref), custom_call_target="tpu_custom_call" | custom-call | tf_op jit(solution)/shard_map/small_gather/pallas_call | solution.py:430
  33.4 2.1 collective-permute-start.1
  36.6 19.5 %team_gather.4 = bf16[8,128,1152]{2,1,0:T(8,128)(2,1)} custom-call(bf16[128,1152]{1,0:T(8,128)(2,1)} %get-tuple-element.104.x_ref), custom_call_target="tpu_custom_call" | custom-call | tf_op jit(solution)/shard_map/team_gather/pallas_call | solution.py:252
  58.2 1.5 reshape.454
  59.7 4.4 all-to-all-start.1
  64.1 35.7 %team_gather.6 = bf16[8,128,1152]{2,1,0:T(8,128)(2,1)} custom-call(bf16[128,1152]{1,0:T(8,128)(2,1)} %get-tuple-element.103.x_ref), custom_call_target="tpu_custom_call" | custom-call | tf_op jit(solution)/shard_map/team_gather/pallas_call | solution.py:252
  105.6 1.5 copy.131
  109.8 4.5 fusion.57
  118.1 3.4 fusion.4.q_ref.k_ref.v_ref
  121.6 6.6 %attend.1 = bf16[1024,256]{1,0:T(8,128)(2,1)} custom-call(bf16[1024,768]{1,0:T(8,128)(2,1)} %fusion.4.q_ref.k_ref.v_ref, bf16[1024,768]{1,0:T(8,128)(2,1)} %fusion.4.q_ref.k_ref.v_ref, bf16[1024,768]{1,0:T(8,128)(2,1)} %fusion.4.q_ref.k_ref.v_ref, f32[2,1024,1]{2,1,0:T(8,128)} %copy.118.gcol_ref, f32[2,1,1024]{2,1,0:T(1,128)} %broadcast_in_dim.172.grow_ref), custom_call_target="tpu_custom_call" | custom-call | flops 1073741824 | bytes 2097152 | tf_op jit(solution)/shard_map/attend/pallas_call | solution.py:119
  130.3 2.3 convolution_convert_fusion.3
  132.7 18.9 %team_scatter.4 = f32[128,1152]{1,0:T(8,128)} custom-call(bf16[8,128,1152]{2,1,0:T(8,128)(2,1)} %bitcast.221), custom_call_target="tpu_custom_call" | custom-call | tf_op jit(solution)/shard_map/team_scatter/pallas_call | solution.py:336
  155.1 39.0 %team_gather.5 = bf16[8,128,1152]{2,1,0:T(8,128)(2,1)} custom-call(bf16[128,1152]{1,0:T(8,128)(2,1)} %add_convert_fusion.3.x_ref), custom_call_target="tpu_custom_call" | custom-call | tf_op jit(solution)/shard_map/team_gather/pallas_call | solution.py:252
  194.1 1.4 broadcast_select_fusion.3
  195.6 2.0 broadcast_select_fusion.1
  198.1 3.3 fusion.19
  201.5 3.6 convert_reduce_fusion
  205.0 2.8 convolution_convert_fusion.5
  207.8 3.7 convolution_convert_fusion.1
  211.5 28.0 %team_scatter.6 = f32[128,1152]{1,0:T(8,128)} custom-call(bf16[8,128,1152]{2,1,0:T(8,128)(2,1)} %bitcast.245), custom_call_target="tpu_custom_call" | custom-call | tf_op jit(solution)/shard_map/team_scatter/pallas_call | solution.py:336
  239.5 2.0 multiply_reduce_fusion.9
  243.7 1.5 convert_reduce_fusion.3
  245.2 15.8 %team_gather.7 = bf16[8,128,1152]{2,1,0:T(8,128)(2,1)} custom-call(bf16[128,1152]{1,0:T(8,128)(2,1)} %get-tuple-element.55.x_ref), custom_call_target="tpu_custom_call" | custom-call | tf_op jit(solution)/shard_map/team_gather/pallas_call | solution.py:252
  261.0 3.9 multiply_reduce_fusion
  265.9 1.5 fusion.48
  267.4 12.0 %attend_back.1 = (f32[1024,256]{1,0:T(8,128)}, f32[1024,256]{1,0:T(8,128)}, f32[1024,256]{1,0:T(8,128)}, f32[2,1024,1]{2,1,0:T(8,128)}, f32[2,1,1024]{2,1,0:T(1,128)}) custom-call(bf16[1024,768]{1,0:T(8,128)(2,1)} %fusion.4.q_ref.k_ref.v_ref, bf16[1024,768]{1,0:T(8,128)(2,1)} %fusion.4.q_ref.k_ref.v_ref, bf16[1024,768]{1,0:T(8,128)(2,1)} %fusion.4.q_ref.k_ref.v_ref, ...), custom_call_target="tpu_custom_call" | custom-call | flops 2684354560 | bytes 5242880 | tf_op jit(solution)/shard_map/attend_back/pallas_call | solution.py:136
  279.4 2.2 convert_element_type.227
  281.6 2.8 select_convert_fusion.1
  284.8 4.2 convert_reduce_fusion.4
  289.0 2.7 convolution_convert_fusion.4
  291.7 2.2 copy-done.19
  293.9 4.3 convolution_convert_fusion
  298.2 4.1 convolution_convert_fusion.2
  303.1 1.7 convolution_convert_fusion.6
  307.5 2.8 copy.126
  310.4 2.6 fusion.123
  313.8 2.2 collective-permute-start.7
  316.1 4.0 concatenate.49
  320.2 3.0 pad_maximum_fusion
  323.3 3.1 copy.122
  326.4 4.4 all-to-all-start.2
  330.8 45.3 %team_scatter.7 = f32[128,1152]{1,0:T(8,128)} custom-call(bf16[8,128,1152]{2,1,0:T(8,128)(2,1)} %bitcast.242), custom_call_target="tpu_custom_call" | custom-call | tf_op jit(solution)/shard_map/team_scatter/pallas_call | solution.py:336
  378.7 2.0 fusion.70
  381.3 16.7 %team_scatter.5 = f32[128,1152]{1,0:T(8,128)} custom-call(bf16[8,128,1152]{2,1,0:T(8,128)(2,1)} %bitcast.241), custom_call_target="tpu_custom_call" | custom-call | tf_op jit(solution)/shard_map/team_scatter/pallas_call | solution.py:336
  400.6 2.7 fusion.62
  410.1 9.1 %small_scatter.1 = f32[4,8,128]{2,1,0:T(8,128)} custom-call(f32[16,8,128]{2,1,0:T(8,128)} %bitcast.262), custom_call_target="tpu_custom_call" | custom-call | tf_op jit(solution)/shard_map/small_scatter/pallas_call | solution.py:466
  433.3 15.5 %small_sum.1 = f32[32,8,128]{2,1,0:T(8,128)} custom-call(f32[32,8,128]{2,1,0:T(8,128)} %pad_bitcast_fusion.x_ref), custom_call_target="tpu_custom_call" | custom-call | tf_op jit(solution)/shard_map/small_sum/pallas_call | solution.py:504
  448.8 1.4 fusion.121
  450.3 2.3 fusion.85
  453.2 4.3 all-to-all-start.3
  460.9 2.3 fusion.27
  463.9 2.3 collective-permute-done.8
  467.0 1.6 reduce_sum.362
  468.8 1.9 collective-permute-start.6
  470.7 2.7 reshape.477
  474.6 2.7 reshape.478
  477.8 3.5 collective-permute-done.11
  481.3 2.5 convert_add_fusion.1
  484.4 3.2 all-to-all-done.3
  491.8 2.2 convert_add_fusion.3
  494.0 14.2 %collective-permute-done.9 = bf16[72,4608]{1,0:T(8,128)(2,1)S(1)} collective-permute-done((bf16[72,4608]{1,0:T(8,128)(2,1)S(1)}, bf16[72,4608]{1,0:T(8,128)(2,1)S(1)}, u32[]{:S(2)}, u32[]{:S(2)}) %collective-permute-start.9) | collective-permute-done | bytes 663584 | tf_op jit(solution)/shard_map/ppermute | solution.py:661
  (304 shorter events, 83.2 us)
Async XLA Ops:
  0.6 17.7 %copy-start = (bf16[1152,432]{0,1:T(8,128)(2,1)S(1)}, bf16[1152,432]{0,1:T(8,128)(2,1)}, u32[]{:S(2)}) copy-start(bf16[1152,432]{0,1:T(8,128)(2,1)} %param.20) | copy-start | bytes 2985988
  4.1 7.0 %copy-start.36 = (bf16[2,1152]{1,0:T(2,128)(2,1)S(1)}, bf16[2,1152]{1,0:T(2,128)(2,1)}, u32[]{:S(2)}) copy-start(bf16[2,1152]{1,0:T(2,128)(2,1)} %param.18) | copy-start | bytes 13828
  4.2 10.1 %copy-start.1 = (bf16[4,32,1152]{2,1,0:T(8,128)(2,1)S(1)}, bf16[4,32,1152]{2,1,0:T(8,128)(2,1)}, u32[]{:S(2)}) copy-start(bf16[4,32,1152]{2,1,0:T(8,128)(2,1)} %param.17) | copy-start | bytes 884740
  4.2 10.5 %copy-start.70 = (s32[2]{0:T(128)S(1)}, s32[2]{0:T(128)}, u32[]{:S(2)}) copy-start(s32[2]{0:T(128)} %param.19) | copy-start | bytes 28
  4.2 12.3 %copy-start.38 = (f32[9,1152]{1,0:T(8,128)S(1)}, f32[9,1152]{1,0:T(8,128)}, u32[]{:S(2)}) copy-start(f32[9,1152]{1,0:T(8,128)} %param.25) | copy-start | bytes 124420
  4.2 13.0 %copy-start.57 = (f32[1152]{0:T(1024)S(1)}, f32[1152]{0:T(1024)}, u32[]{:S(2)}) copy-start(f32[1152]{0:T(1024)} %param.26) | copy-start | bytes 13828
  4.2 14.2 %copy-start.65 = (f32[432]{0:T(512)S(1)}, f32[432]{0:T(512)}, u32[]{:S(2)}) copy-start(f32[432]{0:T(512)} %param.21) | copy-start | bytes 5188
  4.7 15.4 %copy-start.71 = (f32[16]{0:T(128)S(1)}, f32[16]{0:T(128)}, u32[]{:S(2)}) copy-start(f32[16]{0:T(128)} %param.24) | copy-start | bytes 196
  4.7 16.1 %copy-start.44 = (f32[4608]{0:T(1024)S(1)}, f32[4608]{0:T(1024)}, u32[]{:S(2)}) copy-start(f32[4608]{0:T(1024)} %param.30) | copy-start | bytes 55300
  4.9 28.6 %copy-start.35 = (bf16[72,1152]{1,0:T(8,128)(2,1)S(1)}, bf16[72,1152]{1,0:T(8,128)(2,1)}, u32[]{:S(2)}) copy-start(bf16[72,1152]{1,0:T(8,128)(2,1)} %param.27) | copy-start | bytes 497668
  4.9 30.7 %copy-start.6 = (bf16[4,32,1152]{2,1,0:T(8,128)(2,1)S(1)}, bf16[4,32,1152]{2,1,0:T(8,128)(2,1)}, u32[]{:S(2)}) copy-start(bf16[4,32,1152]{2,1,0:T(8,128)(2,1)} %param.33) | copy-start | bytes 884740
  5.8 16.4 %all-to-all-start = ((bf16[8,72,434]{2,1,0:T(8,128)(2,1)}), bf16[8,72,434]{2,1,0:T(8,128)(2,1)}, u32[]{:S(2)}, u32[]{:S(2)}) async-start(bf16[8,72,434]{2,1,0:T(8,128)(2,1)} %pad_maximum_fusion.8), calls=%async_computation | async-start | bytes 1179648 | tf_op jit(solution)/shard_map/all_to_all | solution.py:582
  11.2 10.4 %collective-permute-start.4 = (bf16[2,1152]{1,0:T(2,128)(2,1)S(1)}, bf16[2,1152]{1,0:T(2,128)(2,1)S(1)}, u32[]{:S(2)}, u32[]{:S(2)}) collective-permute-start(bf16[2,1152]{1,0:T(2,128)(2,1)S(1)} %fusion.82), channel_id=1, source_target_pairs={{0,16},{16,0},{1,17},{17,1},{2,18},{18,2},{3,19},{19,3},{4,20},{20... | collective-permute-start | bytes 13832 | tf_op jit(solution)/shard_map/ppermute | solution.py:555
  18.7 37.5 %copy-start.25 = (bf16[72,4608]{1,0:T(8,128)(2,1)S(1)}, bf16[72,4608]{1,0:T(8,128)(2,1)}, u32[]{:S(2)}) copy-start(bf16[72,4608]{1,0:T(8,128)(2,1)} %param.29) | copy-start | bytes 1990660
  19.3 36.8 %copy-start.47 = (f32[128]{0:T(128)}, f32[128]{0:T(128)S(1)}, u32[]{:S(2)}) copy-start(f32[128]{0:T(128)S(1)} %div.59) | copy-start | bytes 1540
  20.0 36.2 %copy-start.58 = (f32[128]{0:T(128)}, f32[128]{0:T(128)S(1)}, u32[]{:S(2)}) copy-start(f32[128]{0:T(128)S(1)} %rsqrt.22) | copy-start | bytes 1540
  33.4 68.0 %collective-permute-start.1 = (bf16[72,1152]{1,0:T(8,128)(2,1)S(1)}, bf16[72,1152]{1,0:T(8,128)(2,1)}, u32[]{:S(2)}, u32[]{:S(2)}) collective-permute-start(bf16[72,1152]{1,0:T(8,128)(2,1)S(1)} %copy-done.35), channel_id=1, source_target_pairs={{0,8},{8,0},{1,9},{9,1},{2,10},{10,2},{3,11},{11,3},{4,12},{12,4},... | collective-permute-start | bytes 497672 | tf_op jit(solution)/shard_map/ppermute | solution.py:567
  56.2 47.1 %collective-permute-start = (bf16[8,72,434]{2,1,0:T(8,128)(2,1)}, bf16[8,72,434]{2,1,0:T(8,128)(2,1)}, u32[]{:S(2)}, u32[]{:S(2)}) collective-permute-start(bf16[8,72,434]{2,1,0:T(8,128)(2,1)} %all-to-all-done), channel_id=1, source_target_pairs={{0,8},{8,0},{1,9},{9,1},{2,10},{10,2},{3,11},{11,3},{4,12},{12,4},... | collective-permute-start | bytes 1499912 | tf_op jit(solution)/shard_map/ppermute | solution.py:567
  59.7 93.3 %all-to-all-start.1 = ((bf16[8,72,576]{2,1,0:T(8,128)(2,1)}), bf16[8,72,576]{2,1,0:T(8,128)(2,1)}, u32[]{:S(2)}, u32[]{:S(2)}) async-start(bf16[8,72,576]{2,1,0:T(8,128)(2,1)} %reshape.454), calls=%async_computation.1 | async-start | bytes 1474560 | tf_op jit(solution)/shard_map/all_to_all | solution.py:609
  99.8 94.3 %collective-permute-start.3 = (bf16[288,1152]{1,0:T(8,128)(2,1)}, bf16[288,1152]{1,0:T(8,128)(2,1)}, u32[]{:S(2)}, u32[]{:S(2)}) collective-permute-start(bf16[288,1152]{1,0:T(8,128)(2,1)} %param.31), channel_id=1, source_target_pairs={{0,8},{8,0},{1,9},{9,1},{2,10},{10,2},{3,11},{11,3},{4,12},{12,4},... | collective-permute-start | bytes 1990664 | tf_op jit(solution)/shard_map/ppermute | solution.py:567
  108.4 5.9 %copy-start.18 = (bf16[1152,6,128]{0,2,1:T(8,128)(2,1)}, bf16[1152,6,128]{0,2,1:T(8,128)(2,1)S(1)}, u32[]{:S(2)}) copy-start(bf16[1152,6,128]{0,2,1:T(8,128)(2,1)S(1)} %pad.47) | copy-start | bytes 5308420
  109.8 4.5 copy-start.63
  109.8 4.6 copy-start.69
  121.5 7.9 %copy-start.48 = (f32[256]{0:T(256)S(1)}, f32[256]{0:T(256)}, u32[]{:S(2)}) copy-start(f32[256]{0:T(256)} %get-tuple-element.85) | copy-start | bytes 3076
  121.5 7.9 %copy-start.49 = (f32[256]{0:T(256)S(1)}, f32[256]{0:T(256)}, u32[]{:S(2)}) copy-start(f32[256]{0:T(256)} %get-tuple-element.86) | copy-start | bytes 3076
  121.5 7.9 %copy-start.50 = (f32[256]{0:T(256)S(1)}, f32[256]{0:T(256)}, u32[]{:S(2)}) copy-start(f32[256]{0:T(256)} %get-tuple-element.87) | copy-start | bytes 3076
  121.5 7.9 %copy-start.51 = (f32[256]{0:T(256)S(1)}, f32[256]{0:T(256)}, u32[]{:S(2)}) copy-start(f32[256]{0:T(256)} %get-tuple-element.88) | copy-start | bytes 3076
  121.5 7.9 %copy-start.52 = (f32[256]{0:T(256)S(1)}, f32[256]{0:T(256)}, u32[]{:S(2)}) copy-start(f32[256]{0:T(256)} %get-tuple-element.89) | copy-start | bytes 3076
  121.5 7.9 %copy-start.53 = (f32[256]{0:T(256)S(1)}, f32[256]{0:T(256)}, u32[]{:S(2)}) copy-start(f32[256]{0:T(256)} %get-tuple-element.90) | copy-start | bytes 3076
  121.6 7.9 %copy-start.54 = (f32[256]{0:T(256)S(1)}, f32[256]{0:T(256)}, u32[]{:S(2)}) copy-start(f32[256]{0:T(256)} %get-tuple-element.91) | copy-start | bytes 3076
  121.6 7.9 %copy-start.55 = (f32[256]{0:T(256)S(1)}, f32[256]{0:T(256)}, u32[]{:S(2)}) copy-start(f32[256]{0:T(256)} %get-tuple-element.92) | copy-start | bytes 3076
  121.6 7.9 %copy-start.56 = (f32[256]{0:T(256)S(1)}, f32[256]{0:T(256)}, u32[]{:S(2)}) copy-start(f32[256]{0:T(256)} %get-tuple-element.93) | copy-start | bytes 3076
  121.6 7.9 %copy-start.60 = (f32[256]{0:T(256)S(1)}, f32[256]{0:T(256)}, u32[]{:S(2)}) copy-start(f32[256]{0:T(256)} %pad_bitcast_fusion.2) | copy-start | bytes 3076
  130.3 21.2 %copy-start.37 = (f32[1152]{0:T(1024)S(1)}, f32[1152]{0:T(1024)}, u32[]{:S(2)}) copy-start(f32[1152]{0:T(1024)} %get-tuple-element.80) | copy-start | bytes 13828
  130.3 21.2 %copy-start.39 = (f32[1152]{0:T(1024)S(1)}, f32[1152]{0:T(1024)}, u32[]{:S(2)}) copy-start(f32[1152]{0:T(1024)} %param.28) | copy-start | bytes 13828
  132.6 20.5 %copy-start.41 = (f32[1152]{0:T(1024)S(1)}, f32[1152]{0:T(1024)}, u32[]{:S(2)}) copy-start(f32[1152]{0:T(1024)} %get-tuple-element.76) | copy-start | bytes 13828
  153.0 42.5 %collective-permute-start.2 = (bf16[8,72,576]{2,1,0:T(8,128)(2,1)}, bf16[8,72,576]{2,1,0:T(8,128)(2,1)}, u32[]{:S(2)}, u32[]{:S(2)}) collective-permute-start(bf16[8,72,576]{2,1,0:T(8,128)(2,1)} %all-to-all-done.1), channel_id=1, source_target_pairs={{0,8},{8,0},{1,9},{9,1},{2,10},{10,2},{3,11},{11,3},{4,12},{12,4},... | collective-permute-start | bytes 1990664 | tf_op jit(solution)/shard_map/ppermute | solution.py:567
  195.5 5.9 %copy-start.26 = (bf16[288,1152]{1,0:T(8,128)(2,1)}, bf16[288,1152]{1,0:T(8,128)(2,1)S(1)}, u32[]{:S(2)}) copy-start(bf16[288,1152]{1,0:T(8,128)(2,1)S(1)} %get-tuple-element.62) | copy-start | bytes 1990660
  195.5 5.9 %copy-start.28 = (bf16[288,1152]{1,0:T(8,128)(2,1)}, bf16[288,1152]{1,0:T(8,128)(2,1)S(1)}, u32[]{:S(2)}) copy-start(bf16[288,1152]{1,0:T(8,128)(2,1)S(1)} %get-tuple-element.63) | copy-start | bytes 1990660
  242.9 18.1 %copy-start.9 = (f32[32,32,256]{2,1,0:T(8,128)S(1)}, f32[32,32,256]{2,1,0:T(8,128)}, u32[]{:S(2)}) copy-start(f32[32,32,256]{2,1,0:T(8,128)} %copy-done.8) | copy-start | bytes 3145732
  242.9 22.0 %copy-start.66 = (f32[128]{0:T(128)}, f32[128]{0:T(128)S(1)}, u32[]{:S(2)}) copy-start(f32[128]{0:T(128)S(1)} %negate_multiply_fusion.1) | copy-start | bytes 1540
  279.4 4.9 copy-start.23
  291.7 6.5 %copy-start.7 = (bf16[1152,896]{0,1:T(8,128)(2,1)}, bf16[1152,896]{0,1:T(8,128)(2,1)S(1)}, u32[]{:S(2)}) copy-start(bf16[1152,896]{0,1:T(8,128)(2,1)S(1)} %convolution_convert_fusion.4) | copy-start | bytes 6193156
  298.2 4.9 copy-start.14
  298.2 4.9 copy-start.72
  306.8 154.1 %collective-permute-start.10 = (bf16[288,1152]{1,0:T(8,128)(2,1)}, bf16[288,1152]{1,0:T(8,128)(2,1)}, u32[]{:S(2)}, u32[]{:S(2)}) collective-permute-start(bf16[288,1152]{1,0:T(8,128)(2,1)} %dynamic-slice_bitcast_fusion), channel_id=1, source_target_pairs={{0,8},{8,0},{1,9},{9,1},{2,10},{10,2},{3,11},{11,3},{4,12},{12,4},... | collective-permute-start | bytes 1990664 | tf_op jit(solution)/shard_map/ppermute | solution.py:675
  310.4 5.6 %slice-start = ((bf16[1152,896]{0,1:T(8,128)(2,1)}), bf16[1152,768]{0,1:T(8,128)(2,1)S(1)}, s32[]{:S(2)}) async-start(bf16[1152,896]{0,1:T(8,128)(2,1)} %copy-done.7), calls=%async_computation.4 | async-start | bytes 3538944 | tf_op jit(solution)/shard_map/slice | solution.py:764
  313.8 145.6 %collective-permute-start.7 = (bf16[72,1152]{1,0:T(8,128)(2,1)}, bf16[72,1152]{1,0:T(8,128)(2,1)S(1)}, u32[]{:S(2)}, u32[]{:S(2)}) collective-permute-start(bf16[72,1152]{1,0:T(8,128)(2,1)} %dynamic-slice_bitcast_fusion.1), channel_id=1, source_target_pairs={{0,8},{8,0},{1,9},{9,1},{2,10},{10,2},{3,11},{11,3},{4,12},{12,4},... | collective-permute-start | bytes 497672 | tf_op jit(solution)/shard_map/ppermute | solution.py:675
  326.4 126.9 %all-to-all-start.2 = ((bf16[16,72,434]{2,1,0:T(8,128)(2,1)}), bf16[16,72,434]{2,1,0:T(8,128)(2,1)}, u32[]{:S(2)}, u32[]{:S(2)}) async-start(bf16[16,72,434]{2,1,0:T(8,128)(2,1)} %copy.122), calls=%async_computation.2 | async-start | bytes 2359296 | tf_op jit(solution)/shard_map/all_to_all | solution.py:666
  376.1 24.6 %copy-start.2 = (f32[128,1152]{1,0:T(8,128)S(1)}, f32[128,1152]{1,0:T(8,128)}, u32[]{:S(2)}) copy-start(f32[128,1152]{1,0:T(8,128)} %team_scatter.7) | copy-start | bytes 1769476
  376.1 24.6 %copy-start.3 = (f32[128,1152]{1,0:T(8,128)S(1)}, f32[128,1152]{1,0:T(8,128)}, u32[]{:S(2)}) copy-start(f32[128,1152]{1,0:T(8,128)} %team_scatter.4) | copy-start | bytes 1769476
  376.1 24.6 %copy-start.40 = (f32[1152]{0:T(1024)S(1)}, f32[1152]{0:T(1024)}, u32[]{:S(2)}) copy-start(f32[1152]{0:T(1024)} %param.28) | copy-start | bytes 13828
  398.0 6.7 %copy-start.43 = (f32[1152]{0:T(1024)S(1)}, f32[1152]{0:T(1024)}, u32[]{:S(2)}) copy-start(f32[1152]{0:T(1024)} %get-tuple-element.50) | copy-start | bytes 13828
  398.0 8.0 %copy-start.42 = (f32[1152]{0:T(1024)S(1)}, f32[1152]{0:T(1024)}, u32[]{:S(2)}) copy-start(f32[1152]{0:T(1024)} %get-tuple-element.44) | copy-start | bytes 13828
  403.3 47.0 %copy-start.45 = (bf16[2,1152]{1,0:T(2,128)(2,1)S(1)}, bf16[2,1152]{1,0:T(2,128)(2,1)}, u32[]{:S(2)}) copy-start(bf16[2,1152]{1,0:T(2,128)(2,1)} %get-tuple-element.83) | copy-start | bytes 13828
  403.3 47.0 %copy-start.46 = (bf16[2,1152]{1,0:T(2,128)(2,1)S(1)}, bf16[2,1152]{1,0:T(2,128)(2,1)}, u32[]{:S(2)}) copy-start(bf16[2,1152]{1,0:T(2,128)(2,1)} %get-tuple-element.84) | copy-start | bytes 13828
  450.3 7.2 %copy-start.34 = (f32[32,8,128]{2,1,0:T(8,128)S(1)}, f32[32,8,128]{2,1,0:T(8,128)}, u32[]{:S(2)}) copy-start(f32[32,8,128]{2,1,0:T(8,128)} %small_sum.1) | copy-start | bytes 393220
  450.3 9.2 %copy-start.21 = (bf16[2,72,1152]{2,1,0:T(8,128)(2,1)S(1)}, bf16[2,72,1152]{2,1,0:T(8,128)(2,1)}, u32[]{:S(2)}) copy-start(bf16[2,72,1152]{2,1,0:T(8,128)(2,1)} %copy-done.20) | copy-start | bytes 995332
  453.2 34.4 %all-to-all-start.3 = ((bf16[16,72,576]{2,1,0:T(8,128)(2,1)}), bf16[16,72,576]{2,1,0:T(8,128)(2,1)S(1)}, u32[]{:S(2)}, u32[]{:S(2)}) async-start(bf16[16,72,576]{2,1,0:T(8,128)(2,1)} %bitcast.67), calls=%async_computation.3 | async-start | bytes 2949120 | tf_op jit(solution)/shard_map/all_to_all | solution.py:666
  459.5 6.7 %collective-permute-start.8 = (bf16[72,1152]{1,0:T(8,128)(2,1)S(1)}, bf16[72,1152]{1,0:T(8,128)(2,1)S(1)}, u32[]{:S(2)}, u32[]{:S(2)}) collective-permute-start(bf16[72,1152]{1,0:T(8,128)(2,1)S(1)} %fusion.77), channel_id=1, source_target_pairs={{0,16},{16,0},{1,17},{17,1},{2,18},{18,2},{3,19},{19,3},{4,20},{20... | collective-permute-start | bytes 497672 | tf_op jit(solution)/shard_map/ppermute | solution.py:661
  463.2 18.1 %collective-permute-start.11 = (bf16[288,1152]{1,0:T(8,128)(2,1)}, bf16[288,1152]{1,0:T(8,128)(2,1)}, u32[]{:S(2)}, u32[]{:S(2)}) collective-permute-start(bf16[288,1152]{1,0:T(8,128)(2,1)} %fusion.27), channel_id=1, source_target_pairs={{0,16},{16,0},{1,17},{17,1},{2,18},{18,2},{3,19},{19,3},{4,20},{20... | collective-permute-start | bytes 1990664 | tf_op jit(solution)/shard_map/ppermute | solution.py:661
  468.8 15.0 %collective-permute-start.6 = (bf16[72,16]{0,1:T(8,128)(2,1)S(1)}, bf16[72,16]{0,1:T(8,128)(2,1)S(1)}, u32[]{:S(2)}, u32[]{:S(2)}) collective-permute-start(bf16[72,16]{0,1:T(8,128)(2,1)S(1)} %bitcast.270), channel_id=1, source_target_pairs={{0,16},{16,0},{1,17},{17,1},{2,18},{18,2},{3,19},{19,3},{4,20},{20... | collective-permute-start | bytes 6920 | tf_op jit(solution)/shard_map/ppermute | solution.py:661
  477.3 14.4 %collective-permute-start.5 = (bf16[72,3456]{1,0:T(8,128)(2,1)}, bf16[72,3456]{1,0:T(8,128)(2,1)}, u32[]{:S(2)}, u32[]{:S(2)}) collective-permute-start(bf16[72,3456]{1,0:T(8,128)(2,1)} %reshape.478), channel_id=1, source_target_pairs={{0,16},{16,0},{1,17},{17,1},{2,18},{18,2},{3,19},{19,3},{4,20},{20... | collective-permute-start | bytes 1493000 | tf_op jit(solution)/shard_map/ppermute | solution.py:661
  490.3 17.8 %collective-permute-start.9 = (bf16[72,4608]{1,0:T(8,128)(2,1)S(1)}, bf16[72,4608]{1,0:T(8,128)(2,1)S(1)}, u32[]{:S(2)}, u32[]{:S(2)}) collective-permute-start(bf16[72,4608]{1,0:T(8,128)(2,1)S(1)} %reshape.484), channel_id=1, source_target_pairs={{0,16},{16,0},{1,17},{17,1},{2,18},{18,2},{3,19},{19,3},{4,20},{20... | collective-permute-start | bytes 1990664 | tf_op jit(solution)/shard_map/ppermute | solution.py:661
  (30 other events, 92.0 us)
